TPU v7x, 8 devices: a whole 2x2x1 slice. The times are simulated.
8 devices in a mesh: part: 1 (over z), loc: 2 (over y), grp: 4 (over x, core).
Axes of the slice: x: 2, y: 2, z: 1, core: 2. Of those that a mesh axis runs over, the one named last changes fastest.
Arguments:
- x_rows: bfloat16 [1536, 1024], P(('part', 'grp', 'loc'))
- dy_rows: bfloat16 [1536, 1024], P(('part', 'grp', 'loc'))
- expert_ids: int32 [1536, 8], P(('part', 'grp', 'loc'))
- gate_vals: float32 [1536, 8], P(('part', 'grp', 'loc'))
- w_gate: bfloat16 [128, 1024, 384], P(('part', 'grp', 'loc'))
- w_up: bfloat16 [128, 1024, 384], P(('part', 'grp', 'loc'))
- w_down: bfloat16 [128, 384, 1024], P(('part', 'grp', 'loc'))
Outputs:
- output 1: bfloat16 [1536, 1024], P(('part', 'grp', 'loc'))
- output 2: float32 [1536, 8], P(('part', 'grp', 'loc'))
- output 3: bfloat16 [128, 1024, 384], P(('part', 'grp', 'loc'))
- output 4: bfloat16 [128, 1024, 384], P(('part', 'grp', 'loc'))
- output 5: bfloat16 [128, 384, 1024], P(('part', 'grp', 'loc'))
All inputs are finite; a program needn't handle non-finite values.
Results may differ from a plain program's by a relative error of at most 0.001.
Values are sent between devices in bfloat16 or wider.
A program may use at most 1 GiB of HBM per device.

v0:
```python
import jax
import jax.numpy as jnp
from jax import lax
from jax.sharding import PartitionSpec as P


def slot_table(bin_ids, num_bins, capacity):
    n_items = bin_ids.shape[0]
    item_order = jnp.argsort(bin_ids, stable=True)
    sorted_bins = bin_ids[item_order]
    bin_sizes = jax.ops.segment_sum(jnp.ones_like(bin_ids), bin_ids, num_segments=num_bins + 1)
    bin_starts = jnp.cumsum(bin_sizes) - bin_sizes
    slot_rank = jnp.arange(n_items, dtype=jnp.int32) - bin_starts[sorted_bins]
    dest_slot = jnp.where(sorted_bins < num_bins, sorted_bins * capacity + slot_rank, num_bins * capacity)
    slot_grid = jnp.full((num_bins * capacity + 1,), n_items, jnp.int32).at[dest_slot].set(item_order.astype(jnp.int32))
    return slot_grid[:num_bins * capacity].reshape(num_bins, capacity)


def gather_rows(source, row_index, fill_val):
    return jnp.take(source, row_index, axis=0, mode='fill', fill_value=fill_val)


def first_in_group(dest_group):
    top_k = dest_group.shape[-1]
    same_group = dest_group[..., :, None] == dest_group[..., None, :]
    earlier = jnp.arange(top_k)[None, :] < jnp.arange(top_k)[:, None]
    return same_group, jnp.logical_not(jnp.any(same_group & earlier, axis=-1))


def expert_backward(x_own, dy_own, gate_own, w_gate, w_up, w_down, row_axes, wt_axes):
    up_form = row_axes + 'd,' + wt_axes + 'df->' + row_axes + 'f'
    down_form = row_axes + 'f,' + wt_axes + 'fd->' + row_axes + 'd'
    back_form = row_axes + 'd,' + wt_axes + 'fd->' + row_axes + 'f'
    tr_form = row_axes + 'f,' + wt_axes + 'df->' + row_axes + 'd'
    grad_down = row_axes + 'f,' + row_axes + 'd->' + wt_axes + 'fd'
    grad_up = row_axes + 'd,' + row_axes + 'f->' + wt_axes + 'df'
    pre_gate = jnp.einsum(up_form, x_own, w_gate, preferred_element_type=jnp.float32)
    pre_up = jnp.einsum(up_form, x_own, w_up, preferred_element_type=jnp.float32)
    sig_gate = jax.nn.sigmoid(pre_gate)
    silu_out = pre_gate * sig_gate
    hidden = (silu_out * pre_up).astype(jnp.bfloat16)
    expert_out = jnp.einsum(down_form, hidden, w_down, preferred_element_type=jnp.float32)
    d_gate = jnp.sum(dy_own * expert_out, axis=-1)
    d_out = (gate_own[..., None] * dy_own).astype(jnp.bfloat16)
    d_hidden = jnp.einsum(back_form, d_out, w_down, preferred_element_type=jnp.float32)
    dw_down = jnp.einsum(grad_down, hidden, d_out, preferred_element_type=jnp.float32).astype(jnp.bfloat16)
    d_pre_up = (d_hidden * silu_out).astype(jnp.bfloat16)
    d_pre_gate = (d_hidden * pre_up * sig_gate * (1.0 + pre_gate * (1.0 - sig_gate))).astype(jnp.bfloat16)
    dw_gate = jnp.einsum(grad_up, x_own, d_pre_gate, preferred_element_type=jnp.float32).astype(jnp.bfloat16)
    dw_up = jnp.einsum(grad_up, x_own, d_pre_up, preferred_element_type=jnp.float32).astype(jnp.bfloat16)
    d_x = (jnp.einsum(tr_form, d_pre_gate, w_gate, preferred_element_type=jnp.float32) + jnp.einsum(tr_form, d_pre_up, w_up, preferred_element_type=jnp.float32)).astype(jnp.bfloat16)
    return d_x, d_gate, dw_gate, dw_up, dw_down


def solution(mesh):
    grp_size = mesh.shape['grp']
    loc_size = mesh.shape['loc']
    spec = P(('part', 'grp', 'loc'))

    def device_step(x_rows, dy_rows, expert_ids, gate_vals, w_gate, w_up, w_down):
        n_tok, d_model = x_rows.shape
        top_k = expert_ids.shape[1]
        local_experts = w_gate.shape[0]
        group_experts = local_experts * loc_size
        num_experts = group_experts * grp_size
        group_limit = min(top_k // 2, grp_size)
        group_rows = group_limit * n_tok // grp_size
        src_cap = min(2 * (n_tok * top_k // num_experts), group_rows)
        relay_cap = grp_size * src_cap
        rows_in = grp_size * group_rows
        my_group = lax.axis_index('grp')

        dest_group = expert_ids // group_experts
        same_group, first_slot = first_in_group(dest_group)
        send_items = slot_table(jnp.where(first_slot, dest_group, grp_size).reshape(-1), grp_size, group_rows)
        send_tok = send_items // top_k
        x_recv = lax.all_to_all(gather_rows(x_rows, send_tok, 0), 'grp', 0, 0).reshape(rows_in, d_model)
        dy_recv = lax.all_to_all(gather_rows(dy_rows, send_tok, 0), 'grp', 0, 0).reshape(rows_in, d_model)
        ids_recv = lax.all_to_all(gather_rows(expert_ids, send_tok, -1), 'grp', 0, 0).reshape(rows_in, top_k)
        gate_recv = lax.all_to_all(gather_rows(gate_vals, send_tok, 0), 'grp', 0, 0).reshape(rows_in * top_k)

        local_ids = ids_recv - my_group * group_experts
        is_mine = (local_ids >= 0) & (local_ids < group_experts)
        fan_items = slot_table(jnp.where(is_mine, local_ids, group_experts).reshape(-1), group_experts, relay_cap)
        fan_rows = fan_items // top_k
        own_shape = (loc_size, local_experts, relay_cap)
        x_own = lax.all_to_all(gather_rows(x_recv, fan_rows, 0).reshape(own_shape + (d_model,)), 'loc', 0, 0)
        dy_own = lax.all_to_all(gather_rows(dy_recv, fan_rows, 0).reshape(own_shape + (d_model,)), 'loc', 0, 0)
        gate_own = lax.all_to_all(gather_rows(gate_recv, fan_items, 0).reshape(own_shape), 'loc', 0, 0)

        d_x, d_gate, dw_gate, dw_up, dw_down = expert_backward(x_own, dy_own, gate_own, w_gate, w_up, w_down, 'lec', 'e')

        contrib_back = lax.all_to_all(d_x, 'loc', 0, 0).reshape(group_experts * relay_cap, d_model)
        dgate_back = lax.all_to_all(d_gate, 'loc', 0, 0).reshape(-1)
        group_sum = jax.ops.segment_sum(contrib_back.astype(jnp.float32), fan_rows.reshape(-1), num_segments=rows_in + 1)
        group_part = group_sum[:rows_in].astype(jnp.bfloat16).reshape(grp_size, group_rows, d_model)
        dgate_rel = jax.ops.segment_sum(dgate_back, fan_items.reshape(-1), num_segments=rows_in * top_k + 1)
        dgate_rel = dgate_rel[:rows_in * top_k].reshape(grp_size, group_rows, top_k)
        part_home = lax.all_to_all(group_part, 'grp', 0, 0).reshape(rows_in, d_model)
        dgate_home = lax.all_to_all(dgate_rel, 'grp', 0, 0).reshape(rows_in, top_k)

        home_tok = send_tok.reshape(-1)
        dx_sum = jax.ops.segment_sum(part_home.astype(jnp.float32), home_tok, num_segments=n_tok + 1)
        d_gates = jax.ops.segment_sum(dgate_home, home_tok, num_segments=n_tok + 1)[:n_tok]
        return dx_sum[:n_tok].astype(jnp.bfloat16), d_gates, dw_gate, dw_up, dw_down

    return jax.shard_map(device_step, mesh=mesh, in_specs=(spec,) * 7, out_specs=(spec,) * 5, check_vma=False)
```

profile of v0, /device:TPU:0, one launch (start us, length us, event | category | flops | bytes accessed | tf_op | source)
XLA Modules:
  0.0 652.5 jit_solution(6505049047775196940)
XLA Ops:
  0.7 0.8 add_select_fusion.2
  1.4 0.8 copy.95
  2.3 0.7 broadcast_select_fusion.6
  3.3 5.0 sort.34
  8.3 8.4 %gather_fusion = s32[1536]{0:T(1024)S(1)} fusion(s32[1536]{0:T(1024)S(1)} %reshape.418, s32[2048]{0:T(1024)S(1)} %pad_clamp_fusion), kind=kCustom, calls=%fused_computation.4 | custom fusion | bytes 18432 | tf_op jit(solution)/shard_map/gather | solution.py:10
  16.7 11.1 %scatter_custom_fusion = s32[5]{0:T(128)S(1)} fusion(s32[1536]{0:T(1024)S(1)} %reshape.418, s32[1536]{0:T(1024)S(1)} %broadcast.429, s32[]{:T(128)} %constant.80.clone.1), kind=kCustom, calls=%fused_computation.192 | custom fusion | flops 1536 | bytes 24 | tf_op jit(solution)/shard_map/scatter-add | solution.py:11
  28.7 3.3 fusion.54
  31.9 6.2 scatter_custom_fusion.1
  39.0 1.6 gather_fusion.1
  40.7 0.6 broadcast_select_fusion.5
  41.4 4.6 all-to-all-start
  46.1 2.8 gather_fusion.5
  48.9 3.6 gather_fusion.7
  52.6 1.6 gather_fusion.3
  54.3 3.4 broadcast_select_fusion.3
  57.7 0.6 broadcast_select_fusion.4
  58.3 3.3 all-to-all-start.1
  62.3 43.1 %scatter_custom_fusion.2 = s32[33]{0:T(128)S(1)} fusion(s32[6144]{0:T(1024)S(1)} %bitcast.165, s32[6144]{0:T(1024)S(1)} %broadcast.430, s32[]{:T(128)} %constant.80.clone.1), kind=kCustom, calls=%fused_computation.190 | custom fusion | flops 6144 | bytes 136 | tf_op jit(solution)/shard_map/scatter-add | solution.py:11
  105.7 0.7 fusion.71
  106.4 0.7 fusion.70
  107.1 6.7 %sort.35 = (s32[6144]{0:T(1024)}, s32[6144]{0:T(1024)S(1)}) sort(s32[6144]{0:T(1024)S(1)} %and_select_fusion.1, s32[6144]{0:T(1024)S(1)} %iota.33), dimensions={0}, to_apply=%region_5.6 | sort | flops 79872 | bytes 98304 | tf_op jit(solution)/shard_map/jit(argsort)/sort | solution.py:9
  113.9 34.3 %gather_fusion.2 = s32[6144]{0:T(1024)S(1)} fusion(s32[6144]{0:T(1024)S(1)} %and_select_fusion.1, s32[6144]{0:T(1024)S(1)} %fusion.42), kind=kCustom, calls=%fused_computation.6 | custom fusion | bytes 73728 | tf_op jit(solution)/shard_map/gather | solution.py:10
  148.2 4.4 compare_select_fusion.2
  152.6 1.9 compare_reduce_fusion.25
  154.5 16.4 %select_select_fusion = s32[6144]{0:T(1024)S(1)} fusion(pred[6144]{0:T(1024)(128)(4,1)S(1)} %get-tuple-element.61, pred[6144]{0:T(1024)(128)(4,1)S(1)} %get-tuple-element.60, pred[6144]{0:T(1024)(128)(4,1)S(1)} %get-tuple-element.59, pred[6144]{0:T(1024)(128)(4,1)S(1)} %get-tuple-element.58, pred[6144]{0:T(1024)(128)(4,1)S(1)} %get-tuple-element.57, ...), kind=kLoop, calls=%fused_computation.115 | loop fusion | flops 159744 | bytes 209000 | tf_op jit(solution)/shard_map/gather | solution.py:13
  171.6 3.6 all-to-all-start.3
  175.2 23.0 %scatter_custom_fusion.3 = s32[3073]{0:T(1024)S(1)} fusion(s32[6144]{0:T(1024)S(1)} %bitcast.166, s32[6144]{0:T(1024)S(1)} %get-tuple-element.10, s32[]{:T(128)} %constant.100.clone.1), kind=kCustom, calls=%fused_computation.152 | custom fusion | bytes 12296 | tf_op jit(solution)/shard_map/scatter | solution.py:15
  198.3 3.6 all-to-all-start.5
  202.8 1.7 copy.102
  204.4 1.2 reshape.426
  205.7 17.4 %gather_fusion.4 = f32[3072]{0:T(1024)S(1)} fusion(f32[6144]{0:T(1024)S(1)} %reshape.426, s32[3072]{0:T(1024)S(1)} %broadcast_clamp_fusion.1), kind=kCustom, calls=%fused_computation.8 | custom fusion | bytes 36864 | tf_op jit(solution)/shard_map/jit(_take)/gather | solution.py:20
  223.2 0.6 and_select_fusion.2
  223.8 13.9 %gather_fusion.6 = bf16[3072,1024]{1,0:T(8,128)(2,1)} fusion(bf16[768,1024]{1,0:T(8,128)(2,1)S(1)} %bitcast.149, s32[3072]{0:T(1024)S(1)} %broadcast_clamp_fusion), kind=kCustom, calls=%fused_computation.1.clone | custom fusion | bytes 12595200 | tf_op jit(solution)/shard_map/jit(_take)/gather | solution.py:20
  237.7 3.3 all-to-all-start.2
  241.0 13.9 %gather_fusion.8 = bf16[3072,1024]{1,0:T(8,128)(2,1)} fusion(bf16[768,1024]{1,0:T(8,128)(2,1)S(1)} %bitcast.150, s32[3072]{0:T(1024)S(1)} %broadcast_clamp_fusion), kind=kCustom, calls=%fused_computation.3.clone | custom fusion | bytes 12595200 | tf_op jit(solution)/shard_map/jit(_take)/gather | solution.py:20
  254.8 10.3 %broadcast_select_fusion.1 = (bf16[32,96,1024]{2,1,0:T(8,128)(2,1)}, bf16[32,96,1024]{2,1,0:T(8,128)(2,1)}) fusion(bf16[32,96,1024]{2,1,0:T(8,128)(2,1)} %bitcast.153, pred[32,96]{1,0:T(8,128)(4,1)S(1)} %get-tuple-element.62, bf16[32,96,1024]{2,1,0:T(8,128)(2,1)} %bitcast.154), kind=kLoop, calls=%fused_computation.41 | loop fusion | flops 6291456 | bytes 25168896 | tf_op jit(solution)/shard_map/jit(_take)/select_n | solution.py:20
  265.2 79.9 %all_to_all.55 = bf16[2,16,96,1024]{3,2,1,0:T(8,128)(2,1)} all-to-all(bf16[2,16,96,1024]{3,2,1,0:T(8,128)(2,1)} %bitcast.152), channel_id=1, replica_groups=mesh['part'=1,'loc'=2,'grp'=4] {'loc'}, dimensions={0} | all-to-all | bytes 12582912 | tf_op jit(solution)/shard_map/all_to_all | solution.py:87
  345.1 6.7 %all-to-all-start.4 = ((bf16[2,16,96,1024]{3,2,1,0:T(8,128)(2,1)}), bf16[2,16,96,1024]{3,2,1,0:T(8,128)(2,1)}, u32[]{:S(2)}, u32[]{:S(2)}) async-start(bf16[2,16,96,1024]{3,2,1,0:T(8,128)(2,1)} %bitcast.151), calls=%async_computation.4 | async-start | bytes 12582912 | tf_op jit(solution)/shard_map/all_to_all | solution.py:88
  351.9 12.0 %fusion.6 = f32[16,2,96,384]{3,2,1,0:T(8,128)} fusion(bf16[16,1024,384]{2,1,0:T(8,128)(2,1)} %param.15, bf16[2,16,96,1024]{3,2,1,0:T(8,128)(2,1)} %all_to_all.55), kind=kOutput, calls=%fused_computation.28 | convolution fusion | flops 2415919104 | bytes 23592960 | tf_op jit(solution)/shard_map/lecd,edf->lecf/dot_general | solution.py:37
  363.9 57.9 %all-to-all-done.4 = bf16[2,16,96,1024]{3,2,1,0:T(8,128)(2,1)} async-done(((bf16[2,16,96,1024]{3,2,1,0:T(8,128)(2,1)}), bf16[2,16,96,1024]{3,2,1,0:T(8,128)(2,1)}, u32[]{:S(2)}, u32[]{:S(2)}) %all-to-all-start.4) | async-done | bytes 6291488 | tf_op jit(solution)/shard_map/all_to_all | solution.py:88
  421.8 12.8 %fusion.10 = f32[16,2,96,384]{3,2,1,0:T(8,128)} fusion(bf16[16,384,1024]{2,1,0:T(8,128)(2,1)} %param.17, f32[2,16,96]{2,0,1:T(2,128)S(1)} %copy.103, bf16[2,16,96,1024]{3,2,1,0:T(8,128)(2,1)} %all-to-all-done.4), kind=kOutput, calls=%fused_computation.32 | convolution fusion | flops 2425356288 | bytes 23605248 | tf_op jit(solution)/shard_map/lecd,efd->lecf/dot_general | solution.py:45
  434.5 13.8 %fusion.28 = (bf16[2,16,96,384]{3,2,0,1:T(8,128)(2,1)}, bf16[2,16,96,384]{3,2,0,1:T(8,128)(2,1)S(1)}, bf16[2,16,96,384]{3,2,0,1:T(8,128)(2,1)}) fusion(f32[16,2,96,384]{3,2,1,0:T(8,128)} %fusion.6, f32[16,2,96,384]{3,2,1,0:T(8,128)} %fusion.10, bf16[16,1024,384]{2,1,0:T(8,128)(2,1)} %param.16, bf16[2,16,96,1024]{3,2,1,0:T(8,128)(2,1)} %all_to_all.55), kind=kOutput, calls=%fused_computation.56 | convolution fusion | flops 2433613824 | bytes 35389440 | tf_op jit(solution)/shard_map/lecd,edf->lecf/dot_general | solution.py:38
  448.3 13.8 %fusion.4 = f32[16,2,96,1024]{3,2,1,0:T(8,128)} fusion(bf16[2,16,96,384]{3,2,0,1:T(8,128)(2,1)S(1)} %get-tuple-element.69, bf16[16,1024,384]{2,1,0:T(8,128)(2,1)} %param.15), kind=kOutput, calls=%fused_computation.26 | convolution fusion | flops 2415919104 | bytes 27525120 | tf_op jit(solution)/shard_map/lecf,edf->lecd/dot_general | solution.py:51
  462.2 10.6 %fusion.1 = f32[2,16,96]{2,0,1:T(2,128)S(1)} fusion(bf16[2,16,96,1024]{3,2,1,0:T(8,128)(2,1)} %all-to-all-done.4, bf16[2,16,96,384]{3,2,0,1:T(8,128)(2,1)} %get-tuple-element.68, bf16[16,384,1024]{2,1,0:T(8,128)(2,1)} %param.17), kind=kOutput, calls=%fused_computation.23 | convolution fusion | flops 2425353216 | bytes 21245952 | tf_op jit(solution)/shard_map/lecf,efd->lecd/dot_general | solution.py:42
  472.8 0.6 copy.108
  473.4 3.2 all-to-all-start.9
  476.6 13.3 %fusion.16 = bf16[2,16,96,1024]{3,2,0,1:T(8,128)(2,1)} fusion(f32[16,2,96,1024]{3,2,1,0:T(8,128)} %fusion.4, bf16[2,16,96,384]{3,2,0,1:T(8,128)(2,1)} %get-tuple-element.70, bf16[16,1024,384]{2,1,0:T(8,128)(2,1)} %param.16), kind=kOutput, calls=%fused_computation.39 | convolution fusion | flops 2422210560 | bytes 33816576 | tf_op jit(solution)/shard_map/lecf,edf->lecd/dot_general | solution.py:51
  489.9 6.6 %copy.107 = bf16[2,16,96,1024]{3,2,1,0:T(8,128)(2,1)} copy(bf16[2,16,96,1024]{3,2,0,1:T(8,128)(2,1)} %fusion.16) | data formatting | bytes 12582912 | tf_op jit(solution)/shard_map/convert_element_type | solution.py:51
  496.6 6.5 all-to-all-start.7
  503.1 12.0 %bitcast_convert_fusion = bf16[16,384,1024]{2,1,0:T(8,128)(2,1)} fusion(bf16[2,16,96,384]{3,2,0,1:T(8,128)(2,1)} %get-tuple-element.68, f32[2,16,96]{2,0,1:T(2,128)S(1)} %copy.103, bf16[2,16,96,1024]{3,2,1,0:T(8,128)(2,1)} %all-to-all-done.4), kind=kOutput, calls=%fused_computation.17 | convolution fusion | flops 2431647744 | bytes 21245952 | tf_op jit(solution)/shard_map/lecf,lecd->efd/dot_general | solution.py:46
  515.2 20.9 %scatter_custom_fusion.6 = f32[6145]{0:T(1024)S(1)} fusion(s32[3072]{0:T(1024)S(1)} %get-tuple-element.71, f32[3072]{0:T(1024)S(1)} %reshape.616, f32[]{:T(128)} %constant.71.clone.1), kind=kCustom, calls=%fused_computation.139 | custom fusion | flops 3072 | bytes 24584 | tf_op jit(solution)/shard_map/scatter-add | solution.py:97
  536.3 0.8 copy.109
  537.1 35.2 %all-to-all-done.7 = bf16[2,16,96,1024]{3,2,1,0:T(8,128)(2,1)} async-done(((bf16[2,16,96,1024]{3,2,1,0:T(8,128)(2,1)}), bf16[2,16,96,1024]{3,2,1,0:T(8,128)(2,1)}, u32[]{:S(2)}, u32[]{:S(2)}) %all-to-all-start.7) | async-done | bytes 6291488 | tf_op jit(solution)/shard_map/all_to_all | solution.py:93
  572.3 3.3 all-to-all-start.10
  575.5 9.6 %bitcast_convert_fusion.2 = bf16[16,1024,384]{2,1,0:T(8,128)(2,1)} fusion(bf16[2,16,96,1024]{3,2,1,0:T(8,128)(2,1)} %all_to_all.55, bf16[2,16,96,384]{3,2,0,1:T(8,128)(2,1)S(1)} %get-tuple-element.69), kind=kOutput, calls=%fused_computation.19 | convolution fusion | flops 2422210560 | bytes 21233664 | tf_op jit(solution)/shard_map/lecd,lecf->edf/dot_general | solution.py:49
  585.1 28.4 %scatter_custom_fusion.4 = f32[769,1024]{1,0:T(8,128)} fusion(s32[3072]{0:T(1024)} %get-tuple-element.72, bf16[3072,1024]{1,0:T(8,128)(2,1)} %bitcast.78, f32[]{:T(128)} %constant.71.clone.1), kind=kCustom, calls=%fused_computation.24 | custom fusion | flops 6291456 | bytes 9441792 | tf_op jit(solution)/shard_map/scatter-add | solution.py:95
  613.5 3.4 slice.93
  616.9 4.6 all-to-all-start.8
  621.6 9.6 %bitcast_convert_fusion.1 = bf16[16,1024,384]{2,1,0:T(8,128)(2,1)} fusion(bf16[2,16,96,1024]{3,2,1,0:T(8,128)(2,1)} %all_to_all.55, bf16[2,16,96,384]{3,2,0,1:T(8,128)(2,1)S(1)} %copy-done.3), kind=kOutput, calls=%fused_computation.18 | convolution fusion | flops 2422210560 | bytes 21233664 | tf_op jit(solution)/shard_map/lecd,lecf->edf/dot_general | solution.py:50
  631.4 6.2 scatter_custom_fusion.7
  637.5 0.7 copy.114
  638.2 3.1 all-to-all-done.8
  641.3 9.9 %scatter_custom_fusion.5 = f32[193,1024]{1,0:T(8,128)S(1)} fusion(s32[768]{0:T(1024)} %get-tuple-element.76, bf16[768,1024]{1,0:T(8,128)(2,1)} %bitcast.79, f32[]{:T(128)} %constant.71.clone.1), kind=kCustom, calls=%fused_computation.60 | custom fusion | flops 1572864 | bytes 2363904 | tf_op jit(solution)/shard_map/scatter-add | solution.py:103
  651.2 0.8 slice.94
  (73 shorter events, 5.7 us)
Async XLA Ops:
  0.6 45.4 %copy-start = (bf16[192,1024]{1,0:T(8,128)(2,1)S(1)}, bf16[192,1024]{1,0:T(8,128)(2,1)}, u32[]{:S(2)}) copy-start(bf16[192,1024]{1,0:T(8,128)(2,1)} %param.12) | copy-start | bytes 1179652
  41.4 16.9 %all-to-all-start = ((s32[4,192,8]{1,2,0:T(8,128)}), s32[4,192,8]{1,2,0:T(8,128)S(1)}, u32[]{:S(2)}, u32[]{:S(2)}) async-start(s32[4,192,8]{1,2,0:T(8,128)} %broadcast_select_fusion.5), calls=%async_computation | async-start | bytes 65536 | tf_op jit(solution)/shard_map/all_to_all | solution.py:79
  46.1 2.8 copy-start.2
  48.9 3.6 copy-start.5
  58.3 112.7 %all-to-all-start.1 = ((f32[4,192,8]{1,2,0:T(8,128)}), f32[4,192,8]{1,2,0:T(8,128)S(1)}, u32[]{:S(2)}, u32[]{:S(2)}) async-start(f32[4,192,8]{1,2,0:T(8,128)} %broadcast_select_fusion.4), calls=%async_computation.1 | async-start | bytes 65536 | tf_op jit(solution)/shard_map/all_to_all | solution.py:80
  171.0 0.6 copy-start.4
  171.6 26.6 %all-to-all-start.3 = ((bf16[4,192,1024]{2,1,0:T(8,128)(2,1)}), bf16[4,192,1024]{2,1,0:T(8,128)(2,1)S(1)}, u32[]{:S(2)}, u32[]{:S(2)}) async-start(bf16[4,192,1024]{2,1,0:T(8,128)(2,1)} %get-tuple-element.77), calls=%async_computation.3 | async-start | bytes 3145728 | tf_op jit(solution)/shard_map/all_to_all | solution.py:78
  198.3 39.4 %all-to-all-start.5 = ((bf16[4,192,1024]{2,1,0:T(8,128)(2,1)}), bf16[4,192,1024]{2,1,0:T(8,128)(2,1)S(1)}, u32[]{:S(2)}, u32[]{:S(2)}) async-start(bf16[4,192,1024]{2,1,0:T(8,128)(2,1)} %get-tuple-element.78), calls=%async_computation.5 | async-start | bytes 3145728 | tf_op jit(solution)/shard_map/all_to_all | solution.py:77
  237.7 27.5 %all-to-all-start.2 = ((f32[2,16,96]{2,1,0:T(8,128)}), f32[2,16,96]{2,1,0:T(8,128)S(1)}, u32[]{:S(2)}, u32[]{:S(2)}) async-start(f32[2,16,96]{2,1,0:T(8,128)} %and_select_fusion.2), calls=%async_computation.2 | async-start | bytes 32768 | tf_op jit(solution)/shard_map/all_to_all | solution.py:89
  345.1 76.7 %all-to-all-start.4 = ((bf16[2,16,96,1024]{3,2,1,0:T(8,128)(2,1)}), bf16[2,16,96,1024]{3,2,1,0:T(8,128)(2,1)}, u32[]{:S(2)}, u32[]{:S(2)}) async-start(bf16[2,16,96,1024]{3,2,1,0:T(8,128)(2,1)} %bitcast.151), calls=%async_computation.4 | async-start | bytes 12582912 | tf_op jit(solution)/shard_map/all_to_all | solution.py:88
  473.4 23.2 %all-to-all-start.9 = ((f32[2,16,96]{2,1,0:T(8,128)}), f32[2,16,96]{2,1,0:T(8,128)S(1)}, u32[]{:S(2)}, u32[]{:S(2)}) async-start(f32[2,16,96]{2,1,0:T(8,128)} %copy.108), calls=%async_computation.9 | async-start | bytes 32768 | tf_op jit(solution)/shard_map/all_to_all | solution.py:94
  496.6 75.7 %all-to-all-start.7 = ((bf16[2,16,96,1024]{3,2,1,0:T(8,128)(2,1)}), bf16[2,16,96,1024]{3,2,1,0:T(8,128)(2,1)}, u32[]{:S(2)}, u32[]{:S(2)}) async-start(bf16[2,16,96,1024]{3,2,1,0:T(8,128)(2,1)} %copy.107), calls=%async_computation.7 | async-start | bytes 12582912 | tf_op jit(solution)/shard_map/all_to_all | solution.py:93
  572.3 44.7 %all-to-all-start.10 = ((f32[4,192,8]{1,2,0:T(8,128)}), f32[4,192,8]{1,2,0:T(8,128)S(1)}, u32[]{:S(2)}, u32[]{:S(2)}) async-start(f32[4,192,8]{1,2,0:T(8,128)} %copy.109), calls=%async_computation.10 | async-start | bytes 65536 | tf_op jit(solution)/shard_map/all_to_all | solution.py:100
  585.1 36.4 %copy-start.3 = (bf16[2,16,96,384]{3,2,0,1:T(8,128)(2,1)S(1)}, bf16[2,16,96,384]{3,2,0,1:T(8,128)(2,1)}, u32[]{:S(2)}) copy-start(bf16[2,16,96,384]{3,2,0,1:T(8,128)(2,1)} %get-tuple-element.70) | copy-start | bytes 7077892
  616.9 24.4 %all-to-all-start.8 = ((bf16[4,192,1024]{2,1,0:T(8,128)(2,1)}), bf16[4,192,1024]{2,1,0:T(8,128)(2,1)}, u32[]{:S(2)}, u32[]{:S(2)}) async-start(bf16[4,192,1024]{2,1,0:T(8,128)(2,1)} %bitcast.155), calls=%async_computation.8 | async-start | bytes 3145728 | tf_op jit(solution)/shard_map/all_to_all | solution.py:99
  621.6 30.5 %copy-start.1 = (bf16[192,1024]{1,0:T(8,128)(2,1)S(1)}, bf16[192,1024]{1,0:T(8,128)(2,1)}, u32[]{:S(2)}) copy-start(bf16[192,1024]{1,0:T(8,128)(2,1)} %param.12) | copy-start | bytes 1179652
where the time goes:
time: 660 us; the launch traced here: 652 us
  other arithmetic  176 us (27%)
  local copies, waits for them, and re-layouts  148 us (22%)
  matrix products  108 us (16%)
  waiting for transfers between devices  96.2 us (15%)
  blocking collectives  79.9 us (12%)
  starting transfers between devices  42.7 us (6%)
    all_to_all x1, blocking collectives, device_step(): lax.all_to_all(gather_rows(x_recv, fan_rows, 0).reshape(own_shape + (d_mo...  79.9 us
    all_to_all x1, waiting for transfers between devices, device_step(): lax.all_to_all(gather_rows(dy_recv, fan_rows, 0).reshape(own_shape + (d_m...  57.9 us
    gather x10, local copies, waits for them, and re-layouts, gather_rows(): return jnp.take(source, row_index, axis=0, mode='fill', fill_value=fill_val)  55 us
    scatter-add x2, other arithmetic, slot_table(): jax.ops.segment_sum(jnp.ones_like(bin_ids), bin_ids, num_segments=num_bin...  54.2 us
    gather x2, local copies, waits for them, and re-layouts, slot_table(): sorted_bins = bin_ids[item_order]  42.7 us
    all_to_all x1, waiting for transfers between devices, device_step(): lax.all_to_all(d_x, 'loc', 0, 0).reshape(group_experts * relay_cap, d_model)  35.2 us
    scatter x2, local copies, waits for them, and re-layouts, slot_table(): jnp.full((num_bins * capacity + 1,), n_items, jnp.int32).at[dest_slot]  29.2 us
    scatter-add x1, other arithmetic, device_step(): jax.ops.segment_sum(contrib_back.astype(jnp.float32), fan_rows.reshape(-1...  28.4 us
  transfers between devices with their start and end apart: 10, of which 3 were waited for; matrix products, arithmetic and copies ran while one was open for 50% of the time, Pallas kernels for 0%

commit v1 on v0

v1 whole, which is shorter than its diff:
```python
import functools

import jax
import jax.numpy as jnp
from jax import lax
from jax.experimental import pallas as pl
from jax.experimental.pallas import tpu as pltpu
from jax.sharding import PartitionSpec as P

N_DEV = 8
N_TOK = 192
D = 1024
F = 384
TOP_K = 8
LOC_E = 16
CAP = 24
SLOTS = N_DEV * CAP
PAIR = 2 * CAP
PAIR_ROWS = LOC_E * PAIR
MESH = pl.DeviceIdType.MESH
F32 = jnp.float32
BF16 = jnp.bfloat16
ANY = pl.BlockSpec(memory_space=pl.ANY)
VMEM = pl.BlockSpec(memory_space=pltpu.VMEM)


def dev_id(g, l):
    return {'grp': g, 'loc': l}


def index_of(g, l):
    return g * 2 + l


def coords():
    g = lax.axis_index('grp')
    l = lax.axis_index('loc')
    core = lax.rem(g, 2)
    gp = g + 1 - 2 * core
    gx = lax.rem(g + 2, 4)
    gxp = lax.rem(gp + 2, 4)
    ly = 1 - l
    return g, l, gp, gx, gxp, ly


def all_barrier(g, l):
    barrier = pltpu.get_barrier_semaphore()
    for k in range(1, N_DEV):
        pl.semaphore_signal(barrier, inc=1, device_id=dev_id(lax.rem(g + k // 2, 4), lax.rem(l + k % 2, 2)), device_id_type=MESH)
    pl.semaphore_wait(barrier, N_DEV - 1)


def gather_kernel(x_ref, dy_ref, meta_ref, xa_ref, dya_ref, ma_ref, send_sem, recv_sem, meta_send, meta_recv, own_sem):
    g, l, gp, gx, gxp, ly = coords()
    me = index_of(g, l)
    role_dev = [me, index_of(gx, l), index_of(g, ly), index_of(gx, ly),
                index_of(gp, l), index_of(gxp, l), index_of(gp, ly), index_of(gxp, ly)]
    to_x, to_y, to_p = dev_id(gx, l), dev_id(g, ly), dev_id(gp, l)
    n_chunk = 4
    half = N_TOK // 2

    def piece(k, src_dev):
        ref = xa_ref if k < 2 else dya_ref
        return ref.at[src_dev, pl.ds((k % 2) * half, half)]

    def own_piece(k):
        ref = x_ref if k < 2 else dy_ref
        return ref.at[pl.ds((k % 2) * half, half)]

    sends = []

    def send(k, src_role, dst_role, target):
        src = own_piece(k) if src_role == 0 else piece(k, role_dev[src_role])
        copy = pltpu.make_async_remote_copy(
            src_ref=src, dst_ref=piece(k, role_dev[src_role]), send_sem=send_sem.at[len(sends)],
            recv_sem=recv_sem.at[dst_role, k], device_id=target, device_id_type=MESH)
        copy.start()
        sends.append(copy)

    def wait_role(role, k):
        pltpu.make_async_remote_copy(
            src_ref=own_piece(k), dst_ref=piece(k, role_dev[role]), send_sem=send_sem.at[0],
            recv_sem=recv_sem.at[role, k], device_id=to_p, device_id_type=MESH).wait_recv()

    own = [pltpu.make_async_copy(x_ref, xa_ref.at[me], own_sem.at[0]),
           pltpu.make_async_copy(dy_ref, dya_ref.at[me], own_sem.at[1]),
           pltpu.make_async_copy(meta_ref, ma_ref.at[me], own_sem.at[2])]
    for copy in own:
        copy.start()
    all_barrier(g, l)
    metas = []
    for i in range(1, N_DEV):
        tg, tl = lax.rem(g + i // 2, 4), lax.rem(l + i % 2, 2)
        copy = pltpu.make_async_remote_copy(
            src_ref=meta_ref, dst_ref=ma_ref.at[me], send_sem=meta_send.at[i], recv_sem=meta_recv.at[i],
            device_id=dev_id(tg, tl), device_id_type=MESH)
        copy.start()
        metas.append(copy)
    for k in range(n_chunk):
        send(k, 0, 1, to_x)
        send(k, 0, 2, to_y)
        send(k, 0, 4, to_p)
    for k in range(n_chunk):
        wait_role(1, k)
        if k % 2 == 0:
            send(k, 1, 3, to_y)
        send(k, 1, 5, to_p)
        wait_role(2, k)
        if k % 2 == 1:
            send(k, 2, 3, to_x)
        send(k, 2, 6, to_p)
    for k in range(n_chunk):
        wait_role(3, k)
        send(k, 3, 7, to_p)
    for k in range(n_chunk):
        for role in range(4, 8):
            wait_role(role, k)
    for i in range(1, N_DEV):
        sg, sl = lax.rem(g + 4 - i // 2, 4), lax.rem(l + i % 2, 2)
        pltpu.make_async_remote_copy(
            src_ref=meta_ref, dst_ref=ma_ref.at[index_of(sg, sl)], send_sem=meta_send.at[i], recv_sem=meta_recv.at[i],
            device_id=dev_id(sg, sl), device_id_type=MESH).wait_recv()
    for copy in metas + sends:
        copy.wait_send()
    for copy in own:
        copy.wait()


def dispatch(x_rows, dy_rows, meta):
    return pl.pallas_call(
        gather_kernel,
        out_shape=[jax.ShapeDtypeStruct((N_DEV, N_TOK, D), BF16), jax.ShapeDtypeStruct((N_DEV, N_TOK, D), BF16),
                   jax.ShapeDtypeStruct((N_DEV, 2 * TOP_K, N_TOK), F32)],
        in_specs=[ANY] * 3, out_specs=[ANY] * 3,
        scratch_shapes=[pltpu.SemaphoreType.DMA((28,)), pltpu.SemaphoreType.DMA((8, 4)), pltpu.SemaphoreType.DMA((8,)),
                        pltpu.SemaphoreType.DMA((8,)), pltpu.SemaphoreType.DMA((3,))],
        compiler_params=pltpu.CompilerParams(collective_id=0, has_side_effects=True),
        name='dispatch',
    )(x_rows, dy_rows, meta)


def dot(a, b, ca=1, cb=0):
    return lax.dot_general(a, b, (((ca,), (cb,)), ((), ())), preferred_element_type=F32)


def slot_iota(rows):
    return lax.broadcasted_iota(jnp.int32, (LOC_E, rows, N_TOK), 1).astype(F32)


def expert_kernel(xa_ref, dya_ref, ma_ref, wg_ref, wu_ref, wd_ref, dwg_ref, dwu_ref, dwd_ref, part_ref, dgate_ref,
                  xs, uds, cs, rank_s, dgs):
    e = pl.program_id(0)

    @pl.when(e == 0)
    def _():
        base = (index_of(lax.axis_index('grp'), lax.axis_index('loc')) * LOC_E).astype(F32)
        e_iota = lax.broadcasted_iota(jnp.int32, (LOC_E, N_TOK), 0).astype(F32) + base
        before = (lax.broadcasted_iota(jnp.int32, (N_TOK, N_TOK), 0) < lax.broadcasted_iota(jnp.int32, (N_TOK, N_TOK), 1)).astype(BF16)

        @pl.loop(0, N_DEV // 2)
        def _(p):
            row0 = pl.multiple_of(p * PAIR, 16)
            hots, gcols = [], []
            for h in range(2):
                d = p * 2 + h
                member = jnp.zeros((LOC_E, N_TOK), F32)
                gate = jnp.zeros((LOC_E, N_TOK), F32)
                for j in range(TOP_K):
                    hit = ma_ref[d, pl.ds(j, 1), :] == e_iota
                    member = jnp.where(hit, 1.0, member)
                    gate = jnp.where(hit, ma_ref[d, pl.ds(TOP_K + j, 1), :], gate)
                rank = jnp.where(member > 0, dot(member.astype(BF16), before), -1000.0)
                rank_s[d] = rank
                mask = rank[:, None, :] == slot_iota(CAP)
                gcols.append(jnp.sum(jnp.where(mask, gate[:, None, :], 0.0), axis=2, keepdims=True))
                hots.append(jnp.where(mask, 1.0, 0.0).reshape(LOC_E * CAP, N_TOK).astype(BF16))
            gcol = jnp.concatenate(gcols, axis=1)
            for c in range(4):
                cols = slice(c * 256, (c + 1) * 256)
                xv = jnp.concatenate([dot(hots[h], xa_ref[p * 2 + h, :, cols]).reshape(LOC_E, CAP, 256) for h in range(2)], axis=1)
                xs[:, pl.ds(row0, PAIR), cols] = xv.astype(BF16)
                yv = jnp.concatenate([dot(hots[h], dya_ref[p * 2 + h, :, cols]).reshape(LOC_E, CAP, 256) for h in range(2)], axis=1)
                uds[:, pl.ds(row0, PAIR), cols] = (gcol * yv).astype(BF16)
                uds[:, pl.ds(pl.multiple_of(row0 + SLOTS, 16), PAIR), cols] = yv.astype(BF16)

    x = xs[e]
    pre_gate = dot(x, wg_ref[0])
    pre_up = dot(x, wu_ref[0])
    sig = jax.nn.sigmoid(pre_gate)
    silu = pre_gate * sig
    hidden = (silu * pre_up).astype(BF16)
    back = dot(uds[e], wd_ref[0], 1, 1)
    d_hidden = back[:SLOTS]
    dgs[e] = jnp.broadcast_to(jnp.sum(hidden.astype(F32) * back[SLOTS:], axis=1, keepdims=True), (SLOTS, 128))
    d_up = (d_hidden * silu).astype(BF16)
    d_gate = (d_hidden * pre_up * sig * (1.0 + pre_gate * (1.0 - sig))).astype(BF16)
    c = (dot(d_gate, wg_ref[0], 1, 1) + dot(d_up, wu_ref[0], 1, 1)).astype(BF16)
    for p in range(N_DEV // 2):
        cs[p, pl.ds(pl.multiple_of(e * PAIR, 16), PAIR), :] = c[p * PAIR:(p + 1) * PAIR]
    dwd_ref[0] = dot(hidden, uds[e, :SLOTS], 0, 0).astype(BF16)
    dwg_ref[0] = dot(x, d_gate, 0, 0).astype(BF16)
    dwu_ref[0] = dot(x, d_up, 0, 0).astype(BF16)

    @pl.when(e == LOC_E - 1)
    def _():
        @pl.loop(0, N_DEV // 2)
        def _(p):
            for h in range(2):
                d = p * 2 + h
                rank = rank_s[d]
                mask = rank[:, None, :] == slot_iota(CAP)
                vals = dgs[:, pl.ds(pl.multiple_of(p * PAIR + h * CAP, 8), CAP), :][:, :, :1]
                dgate_ref[d] = jnp.sum(jnp.where(mask, vals, 0.0), axis=1)
                wide = (rank + float(h * CAP))[:, None, :] == slot_iota(PAIR)
                hot = jnp.where(wide, 1.0, 0.0).reshape(PAIR_ROWS, N_TOK).astype(BF16)
                for q in range(4):
                    cols = slice(q * 256, (q + 1) * 256)
                    part_ref[d, :, cols] = dot(hot, cs[p, :, cols], 0, 0).astype(BF16)


def expert_stage(xa, dya, meta_all, w_gate, w_up, w_down):
    whole = lambda *shape: pl.BlockSpec(shape, lambda e: (0,) * len(shape), pipeline_mode=pl.Buffered(1))
    each = lambda *shape: pl.BlockSpec((1,) + shape, lambda e: (e, 0, 0))
    return pl.pallas_call(
        expert_kernel,
        grid=(LOC_E,),
        out_shape=[jax.ShapeDtypeStruct((LOC_E, D, F), BF16), jax.ShapeDtypeStruct((LOC_E, D, F), BF16), jax.ShapeDtypeStruct((LOC_E, F, D), BF16),
                   jax.ShapeDtypeStruct((N_DEV, N_TOK, D), BF16), jax.ShapeDtypeStruct((N_DEV, LOC_E, N_TOK), F32)],
        in_specs=[whole(N_DEV, N_TOK, D), whole(N_DEV, N_TOK, D), whole(N_DEV, 2 * TOP_K, N_TOK), each(D, F), each(D, F), each(F, D)],
        out_specs=[each(D, F), each(D, F), each(F, D), whole(N_DEV, N_TOK, D), whole(N_DEV, LOC_E, N_TOK)],
        scratch_shapes=[pltpu.VMEM((LOC_E, SLOTS, D), BF16), pltpu.VMEM((LOC_E, 2 * SLOTS, D), BF16), pltpu.VMEM((N_DEV // 2, PAIR_ROWS, D), BF16),
                        pltpu.VMEM((N_DEV, LOC_E, N_TOK), F32), pltpu.VMEM((LOC_E, SLOTS, 128), F32)],
        compiler_params=pltpu.CompilerParams(vmem_limit_bytes=60 * 1024 * 1024, dimension_semantics=('arbitrary',)),
        name='experts',
    )(xa, dya, meta_all, w_gate, w_up, w_down)


def combine_kernel(part_ref, dgate_ref, ids_ref, dx_ref, dg_ref, pv, dv, send_sem, recv_sem, own_sem):
    g = lax.axis_index('grp')
    l = lax.axis_index('loc')
    me = index_of(g, l)
    own = [pltpu.make_async_copy(part_ref.at[me], pv.at[me], own_sem.at[0]), pltpu.make_async_copy(dgate_ref.at[me], dv.at[me], own_sem.at[1])]
    for copy in own:
        copy.start()
    all_barrier(g, l)
    sends = []
    for i in range(1, N_DEV):
        tg, tl = lax.rem(g + i // 2, 4), lax.rem(l + i % 2, 2)
        them = index_of(tg, tl)
        for a, (src, dst) in enumerate(((dgate_ref, dv), (part_ref, pv))):
            copy = pltpu.make_async_remote_copy(
                src_ref=src.at[them], dst_ref=dst.at[me], send_sem=send_sem.at[i, a], recv_sem=recv_sem.at[i, a],
                device_id=dev_id(tg, tl), device_id_type=MESH)
            copy.start()
            sends.append(copy)
    for i in range(1, N_DEV):
        sg, sl = lax.rem(g + 4 - i // 2, 4), lax.rem(l + i % 2, 2)
        them = index_of(sg, sl)
        for a, (src, dst) in enumerate(((dgate_ref, dv), (part_ref, pv))):
            pltpu.make_async_remote_copy(
                src_ref=src.at[them], dst_ref=dst.at[them], send_sem=send_sem.at[i, a], recv_sem=recv_sem.at[i, a],
                device_id=dev_id(sg, sl), device_id_type=MESH).wait_recv()
    for copy in own:
        copy.wait()
    for copy in sends:
        copy.wait_send()

    @pl.loop(0, N_TOK // 16)
    def _(r):
        rows = pl.ds(pl.multiple_of(r * 16, 16), 16)
        total = jnp.zeros((16, D), F32)
        for q in range(N_DEV // 2):
            total += (pv[2 * q, rows].astype(F32) + pv[2 * q + 1, rows].astype(F32)).astype(BF16).astype(F32)
        dx_ref[rows] = total.astype(BF16)

    e_iota = lax.broadcasted_iota(jnp.int32, (LOC_E, N_TOK), 0)
    for j in range(TOP_K):
        want = ids_ref[pl.ds(j, 1), :]
        acc = jnp.zeros((LOC_E, N_TOK), F32)
        for d in range(N_DEV):
            acc = jnp.where(want == e_iota + d * LOC_E, dv[d], acc)
        dg_ref[pl.ds(j, 1), :] = jnp.sum(acc, axis=0, keepdims=True)


def combine(part, dgate, ids_t):
    return pl.pallas_call(
        combine_kernel,
        out_shape=[jax.ShapeDtypeStruct((N_TOK, D), BF16), jax.ShapeDtypeStruct((TOP_K, N_TOK), F32)],
        in_specs=[ANY, ANY, VMEM], out_specs=[VMEM, VMEM],
        scratch_shapes=[pltpu.VMEM((N_DEV, N_TOK, D), BF16), pltpu.VMEM((N_DEV, LOC_E, N_TOK), F32),
                        pltpu.SemaphoreType.DMA((8, 2)), pltpu.SemaphoreType.DMA((8, 2)), pltpu.SemaphoreType.DMA((2,))],
        compiler_params=pltpu.CompilerParams(collective_id=1, has_side_effects=True, vmem_limit_bytes=32 * 1024 * 1024),
        name='combine',
    )(part, dgate, ids_t)


def solution(mesh):
    spec = P(('part', 'grp', 'loc'))

    def device_step(x_rows, dy_rows, expert_ids, gate_vals, w_gate, w_up, w_down):
        ids_t = expert_ids.T
        meta = jnp.concatenate([ids_t.astype(F32), gate_vals.T], axis=0)
        xa, dya, meta_all = dispatch(x_rows, dy_rows, meta)
        dwg, dwu, dwd, part, dgate = expert_stage(xa, dya, meta_all, w_gate, w_up, w_down)
        dx, dg_t = combine(part, dgate, ids_t)
        return dx, dg_t.T, dwg, dwu, dwd

    return jax.shard_map(device_step, mesh=mesh, in_specs=(spec,) * 7, out_specs=(spec,) * 5, check_vma=False)
```

time: 660 us -> 136 us (0.21)
  other arithmetic: 176 us -> 2.01 us
  local copies, waits for them, and re-layouts: 148 us -> 4.14 us
  Pallas kernels: 0 us -> 127 us
  matrix products: 108 us -> 0 us
  waiting for transfers between devices: 96.2 us -> 0 us
  blocking collectives: 79.9 us -> 0 us
  starting transfers between devices: 42.7 us -> 0 us
    pallas_call x0 -> x3, Pallas kernels: none -> 127 us  [the longest x1 54.1 us: expert_stage(): pl.pallas_call(expert_kernel, grid=(LOC_E,), out_shape=[jax.ShapeDtypeStr...]
    scatter-add x6 -> x0, other arithmetic: 120 us -> none  [the longest x2 54.2 us: slot_table(): jax.ops.segment_sum(jnp.ones_like(bin_ids), bin_ids, num_segments=num_bin...]
    dot_general x9 -> x0, matrix products: 108 us -> none  [the longest x1 13.8 us: expert_backward(): jnp.einsum(tr_form, d_pre_gate, w_gate, preferred_element_type=jnp.float32)]
    gather x15 -> x0, local copies, waits for them, and re-layouts: 99.8 us -> none  [the longest x10 55 us: gather_rows(): return jnp.take(source, row_index, axis=0, mode='fill', fill_value=fill_val)]
    all_to_all x10 -> x0, waiting for transfers between devices: 96.2 us -> none  [the longest x1 57.9 us: device_step(): lax.all_to_all(gather_rows(dy_recv, fan_rows, 0).reshape(own_shape + (d_m...]
    all_to_all x1 -> x0, blocking collectives: 79.9 us -> none  [device_step(): lax.all_to_all(gather_rows(x_recv, fan_rows, 0).reshape(own_shape + (d_mo...]
    all_to_all x10 -> x0, starting transfers between devices: 42.7 us -> none  [the longest x1 6.74 us: device_step(): lax.all_to_all(gather_rows(dy_recv, fan_rows, 0).reshape(own_shape + (d_m...]
    scatter x2 -> x0, local copies, waits for them, and re-layouts: 29.2 us -> none  [slot_table(): jnp.full((num_bins * capacity + 1,), n_items, jnp.int32).at[dest_slot]]
  transfers between devices with their start and end apart: 10 -> 0, of which waited for: 3 -> 0; matrix products, arithmetic and copies ran while one was open for 50% -> 0% of each run, Pallas kernels for 0% -> 0%
where the time goes in v1:
time: 136 us; the launch traced here: 134 us
  Pallas kernels  127 us (93%)
  local copies, waits for them, and re-layouts  4.14 us (3%)
  other arithmetic  2.01 us (1%)
    pallas_call x1, Pallas kernels, expert_stage(): pl.pallas_call(expert_kernel, grid=(LOC_E,), out_shape=[jax.ShapeDtypeStr...  54.1 us
    pallas_call x1, Pallas kernels, combine(): pl.pallas_call(combine_kernel, out_shape=[jax.ShapeDtypeStruct((N_TOK, D)...  38.6 us
    pallas_call x1, Pallas kernels, dispatch(): pl.pallas_call(gather_kernel, out_shape=[jax.ShapeDtypeStruct((N_DEV, N_T...  34.6 us
    unnamed x8, local copies, waits for them, and re-layouts  4.14 us

profile of v1, /device:TPU:0, one launch (start us, length us, event | category | flops | bytes accessed | tf_op | source)
XLA Modules:
  0.0 134.1 jit_solution(5677175587731816567)
XLA Ops:
  0.6 0.7 bitcast_convert_fusion
  1.3 1.3 pad_maximum_fusion.meta_ref
  2.6 34.6 %dispatch.1 = (bf16[8,192,1024]{2,1,0:T(8,128)(2,1)}, bf16[8,192,1024]{2,1,0:T(8,128)(2,1)}, f32[8,16,192]{2,1,0:T(8,128)}) custom-call(bf16[192,1024]{1,0:T(8,128)(2,1)} %x_ref.1, bf16[192,1024]{1,0:T(8,128)(2,1)} %dy_ref.1, f32[16,192]{1,0:T(8,128)} %pad_maximum_fusion.meta_ref), custom_call_target="tpu_custom_call" | custom-call | tf_op jit(solution)/shard_map/dispatch/pallas_call | solution.py:130
  37.2 0.0 copy-start.2
  37.2 54.1 %experts.1 = (bf16[16,1024,384]{2,1,0:T(8,128)(2,1)}, bf16[16,1024,384]{2,1,0:T(8,128)(2,1)}, bf16[16,384,1024]{2,1,0:T(8,128)(2,1)}, bf16[8,192,1024]{2,1,0:T(8,128)(2,1)}, f32[8,16,192]{2,1,0:T(8,128)}) custom-call(bf16[8,192,1024]{2,1,0:T(8,128)(2,1)} %get-tuple-element.15.xa_ref, bf16[8,192,1024]{2,1,0:T(8,128)(2,1)} %get-tuple-element.16.dya_ref, ...), custom_call_target="tpu_custom_call" | custom-call | tf_op jit(solution)/shard_map/experts/pallas_call | solution.py:224
  91.3 0.0 copy-done.2
  91.3 0.0 copy-start
  91.3 1.9 %copy-done = bf16[8,192,1024]{2,1,0:T(8,128)(2,1)S(1)} copy-done((bf16[8,192,1024]{2,1,0:T(8,128)(2,1)S(1)}, bf16[8,192,1024]{2,1,0:T(8,128)(2,1)}, u32[]{:S(2)}) %copy-start) | copy-done | bytes 3145752
  93.2 0.0 copy-start.1
  93.2 0.9 copy-done.1
  94.1 38.6 %combine.1 = (bf16[192,1024]{1,0:T(8,128)(2,1)S(1)}, f32[8,192]{1,0:T(8,128)S(1)}) custom-call(bf16[8,192,1024]{2,1,0:T(8,128)(2,1)S(1)} %copy-done, f32[8,16,192]{2,1,0:T(8,128)S(1)} %copy-done.1, s32[8,192]{1,0:T(8,128)S(1)} %bitcast.4), custom_call_target="tpu_custom_call" | custom-call | tf_op jit(solution)/shard_map/combine/pallas_call | solution.py:286
  132.7 0.7 copy.14
  133.5 0.6 copy.15
Async XLA Ops:
  37.2 54.1 %copy-start.2 = (s32[192,8]{0,1:T(8,128)S(1)}, s32[192,8]{0,1:T(8,128)}, u32[]{:S(2)}) copy-start(s32[192,8]{0,1:T(8,128)} %param.9) | copy-start | bytes 18436
  91.3 1.9 %copy-start = (bf16[8,192,1024]{2,1,0:T(8,128)(2,1)S(1)}, bf16[8,192,1024]{2,1,0:T(8,128)(2,1)}, u32[]{:S(2)}) copy-start(bf16[8,192,1024]{2,1,0:T(8,128)(2,1)} %get-tuple-element.18.part_ref) | copy-start | bytes 9437188
  93.2 0.9 copy-start.1

commit v2 on v0

v2 whole, which is shorter than its diff:
```python
import jax
import jax.numpy as jnp
from jax import lax
from jax.experimental import pallas as pl
from jax.experimental.pallas import tpu as pltpu
from jax.sharding import PartitionSpec as P

N_DEV = 8
N_TOK = 192
HALF = N_TOK // 2
D = 1024
F = 384
TOP_K = 8
LOC_E = 16
CAP = 24
SLOTS = N_DEV * CAP
PAIR = 2 * CAP
PAIR_ROWS = LOC_E * PAIR
N_PAIR = N_DEV // 2
RING = 4
MESH = pl.DeviceIdType.MESH
F32 = jnp.float32
BF16 = jnp.bfloat16
ANY = pl.BlockSpec(memory_space=pl.ANY)
VMEM = pl.BlockSpec(memory_space=pltpu.VMEM)


def dot(a, b, ca=1, cb=0):
    return lax.dot_general(a, b, (((ca,), (cb,)), ((), ())), preferred_element_type=F32)


def role_coords(role):
    g = lax.axis_index('grp')
    l = lax.axis_index('loc')
    if role & 1:
        g = g + 1 - 2 * lax.rem(g, 2)
    if role & 2:
        g = lax.rem(g + 2, 4)
    if role & 4:
        l = 1 - l
    return g, l


def role_id(role):
    g, l = role_coords(role)
    return {'grp': g, 'loc': l}


def role_expert_base(role):
    g, l = role_coords(role)
    return (g * 2 + l) * LOC_E


def slot_iota(rows):
    return lax.broadcasted_iota(jnp.int32, (LOC_E, rows, N_TOK), 1).astype(F32)


def front_kernel(x_ref, dy_ref, meta_ref, wg_ref, wu_ref, wd_ref,
                 part_ref, dgate_ref, xs_ref, us_ref, hid_ref, dab_ref,
                 xa, dya, ma, xs, uds, cs, hots, gcols, ranks, back, dgs, wd_buf, w_buf, hid_st, dab_st, dg_out, dg_in, part_st,
                 send_sem, recv_sem, meta_send, meta_recv, dg_send, dg_recv, own_sem, wd_sem, w_sem, st_sem, out_sem):
    P_, X_, Y_ = 1, 2, 4
    data = (dya, xa)
    raw = (dy_ref, x_ref)
    sends = []

    def piece(a, role, k):
        return data[a].at[role, pl.ds(k * HALF, HALF)]

    def send(a, k, src_role, hop):
        dst_role = src_role ^ hop
        src = raw[a].at[pl.ds(k * HALF, HALF)] if src_role == 0 else piece(a, src_role, k)
        copy = pltpu.make_async_remote_copy(
            src_ref=src, dst_ref=piece(a, dst_role, k), send_sem=send_sem.at[len(sends)],
            recv_sem=recv_sem.at[a, dst_role, k], device_id=role_id(hop), device_id_type=MESH)
        copy.start()
        sends.append(copy)

    def arrived(a, role, k):
        pltpu.make_async_remote_copy(
            src_ref=piece(a, role, k), dst_ref=piece(a, role, k), send_sem=send_sem.at[0],
            recv_sem=recv_sem.at[a, role, k], device_id=role_id(P_), device_id_type=MESH).wait_recv()

    def wd_copy(e):
        slot = lax.rem(e, RING)
        return pltpu.make_async_copy(wd_ref.at[e], wd_buf.at[slot], wd_sem.at[slot])

    def w_copies(e):
        slot = lax.rem(e, RING)
        return (pltpu.make_async_copy(wg_ref.at[e], w_buf.at[slot, :, pl.ds(0, F)], w_sem.at[slot, 0]),
                pltpu.make_async_copy(wu_ref.at[e], w_buf.at[slot, :, pl.ds(F, F)], w_sem.at[slot, 1]))

    own = [pltpu.make_async_copy(meta_ref, ma.at[0], own_sem.at[0]), pltpu.make_async_copy(dy_ref, dya.at[0], own_sem.at[1]),
           pltpu.make_async_copy(x_ref, xa.at[0], own_sem.at[2])]
    for copy in own:
        copy.start()
    for e in range(RING):
        wd_copy(e).start()
    for e in range(RING):
        for copy in w_copies(e):
            copy.start()

    barrier = pltpu.get_barrier_semaphore()
    for role in range(1, N_DEV):
        pl.semaphore_signal(barrier, inc=1, device_id=role_id(role), device_id_type=MESH)
    pl.semaphore_wait(barrier, N_DEV - 1)

    metas = []
    for role in range(1, N_DEV):
        copy = pltpu.make_async_remote_copy(
            src_ref=meta_ref, dst_ref=ma.at[role], send_sem=meta_send.at[role], recv_sem=meta_recv.at[role],
            device_id=role_id(role), device_id_type=MESH)
        copy.start()
        metas.append(copy)
    for k in range(2):
        send(0, k, 0, X_)
        send(0, 1 - k, 0, Y_)
        send(0, k, 0, P_)
    own[0].wait()
    for copy in metas:
        copy.wait_recv()

    e_iota = (lax.broadcasted_iota(jnp.int32, (LOC_E, N_TOK), 0) + role_expert_base(0)).astype(F32)
    before = (lax.broadcasted_iota(jnp.int32, (N_TOK, N_TOK), 0) < lax.broadcasted_iota(jnp.int32, (N_TOK, N_TOK), 1)).astype(BF16)

    @pl.loop(0, N_DEV)
    def _(r):
        member = jnp.zeros((LOC_E, N_TOK), F32)
        gate = jnp.zeros((LOC_E, N_TOK), F32)
        meta = ma[r]
        for j in range(TOP_K):
            hit = meta[j:j + 1] == e_iota
            member = jnp.where(hit, 1.0, member)
            gate = jnp.where(hit, meta[TOP_K + j:TOP_K + j + 1], gate)
        rank = jnp.where(member > 0, dot(member.astype(BF16), before), -1000.0)
        ranks[r] = rank
        mask = rank[:, None, :] == slot_iota(CAP)
        gcol = jnp.sum(jnp.where(mask, gate[:, None, :], 0.0), axis=2, keepdims=True)
        gcols[r] = jnp.broadcast_to(gcol, (LOC_E, CAP, 128))
        hots[r] = jnp.where(mask, 1.0, 0.0).reshape(LOC_E * CAP, N_TOK).astype(BF16)

    def gather(a, q):
        @pl.loop(0, 4)
        def _(c):
            cols = pl.ds(pl.multiple_of(c * 256, 256), 256)
            rows = pl.ds(q * PAIR, PAIR)
            vals = jnp.concatenate([dot(hots[2 * q + h], data[a][2 * q + h, :, cols]).reshape(LOC_E, CAP, 256) for h in range(2)], axis=1)
            if a == 1:
                xs[:, rows, cols] = vals.astype(BF16)
            else:
                gcol = jnp.concatenate([gcols[2 * q + h][:, :, :1] for h in range(2)], axis=1)
                uds[:, rows, cols] = (gcol * vals).astype(BF16)
                uds[:, pl.ds(SLOTS + q * PAIR, PAIR), cols] = vals.astype(BF16)

    def first_relays(a):
        arrived(a, X_, 0)
        send(a, 0, X_, Y_)
        send(a, 0, X_, P_)
        arrived(a, Y_, 1)
        send(a, 1, Y_, X_)
        send(a, 1, Y_, P_)

    def second_forwards(a):
        arrived(a, X_, 1)
        send(a, 1, X_, P_)
        arrived(a, Y_, 0)
        send(a, 0, Y_, P_)

    def last_forwards(a):
        for k in range(2):
            arrived(a, X_ | Y_, k)
            send(a, k, X_ | Y_, P_)

    own[1].wait()
    for k in range(2):
        arrived(0, P_, k)
    gather(0, 0)
    first_relays(0)
    for k in range(2):
        send(1, k, 0, X_)
        send(1, 1 - k, 0, Y_)
        send(1, k, 0, P_)
    own[2].wait()
    second_forwards(0)
    for role in (X_ | P_, Y_ | P_):
        for k in range(2):
            arrived(0, role, k)
    gather(0, 1)
    gather(0, 2)
    for k in range(2):
        arrived(1, P_, k)
    gather(1, 0)
    last_forwards(0)
    for k in range(2):
        arrived(0, X_ | Y_ | P_, k)
    gather(0, 3)
    us_copy = pltpu.make_async_copy(uds.at[:, pl.ds(0, SLOTS)], us_ref, out_sem.at[0])
    us_copy.start()

    def back_step(e):
        slot = lax.rem(e, RING)
        wd_copy(e).wait()
        back[e] = dot(uds[e], wd_buf[slot], 1, 1)

        @pl.when(e + RING < LOC_E)
        def _():
            wd_copy(e + RING).start()

    pl.loop(0, LOC_E // 2)(back_step)
    first_relays(1)
    pl.loop(LOC_E // 2, LOC_E)(back_step)
    second_forwards(1)
    for role in (X_ | P_, Y_ | P_):
        for k in range(2):
            arrived(1, role, k)
    gather(1, 1)
    gather(1, 2)
    last_forwards(1)
    for k in range(2):
        arrived(1, X_ | Y_ | P_, k)
    gather(1, 3)
    xs_copy = pltpu.make_async_copy(xs, xs_ref, out_sem.at[1])
    xs_copy.start()

    def st_copies(e):
        slot = lax.rem(e, 2)
        return (pltpu.make_async_copy(hid_st.at[slot], hid_ref.at[e], st_sem.at[slot, 0]),
                pltpu.make_async_copy(dab_st.at[slot], dab_ref.at[e], st_sem.at[slot, 1]))

    @pl.loop(0, LOC_E)
    def _(e):
        slot = lax.rem(e, RING)
        st = lax.rem(e, 2)
        for copy in w_copies(e):
            copy.wait()

        @pl.when(e >= 2)
        def _():
            for copy in st_copies(e - 2):
                copy.wait()

        pre = dot(xs[e], w_buf[slot])
        pre_gate = pre[:, :F]
        pre_up = pre[:, F:]
        sig = jax.nn.sigmoid(pre_gate)
        silu = pre_gate * sig
        hidden = (silu * pre_up).astype(BF16)
        d_hidden = back[e, :SLOTS]
        dgs[e] = jnp.broadcast_to(jnp.sum(hidden.astype(F32) * back[e, SLOTS:], axis=1, keepdims=True), (SLOTS, 128))
        d_up = (d_hidden * silu).astype(BF16)
        d_gate = (d_hidden * pre_up * sig * (1.0 + pre_gate * (1.0 - sig))).astype(BF16)
        hid_st[st] = hidden
        dab = jnp.concatenate([d_gate, d_up], axis=1)
        dab_st[st] = dab
        for copy in st_copies(e):
            copy.start()
        c = dot(dab, w_buf[slot], 1, 1).astype(BF16)
        for q in range(N_PAIR):
            cs[q, pl.ds(pl.multiple_of(e * PAIR, 16), PAIR), :] = c[q * PAIR:(q + 1) * PAIR]

        @pl.when(e + RING < LOC_E)
        def _():
            for copy in w_copies(e + RING):
                copy.start()

    dg_copies = []
    for r in range(N_DEV):
        mask = ranks[r][:, None, :] == slot_iota(CAP)
        vals = dgs[:, r * CAP:(r + 1) * CAP, :][:, :, :1]
        dg_out[r] = jnp.sum(jnp.where(mask, vals, 0.0), axis=1)
        if r:
            copy = pltpu.make_async_remote_copy(
                src_ref=dg_out.at[r], dst_ref=dg_in.at[r], send_sem=dg_send.at[r], recv_sem=dg_recv.at[r],
                device_id=role_id(r), device_id_type=MESH)
            copy.start()
            dg_copies.append(copy)

    part_copies = []
    for r in range(N_DEV):
        q, h = r // 2, r % 2

        wide = (ranks[r] + float(h * CAP))[:, None, :] == slot_iota(PAIR)
        hot = jnp.where(wide, 1.0, 0.0).reshape(PAIR_ROWS, N_TOK).astype(BF16)
        for c in range(4):
            cols = slice(c * 256, (c + 1) * 256)
            part_st[r, :, cols] = dot(hot, cs[q, :, cols], 0, 0).astype(BF16)
        g, l = role_coords(r)
        copy = pltpu.make_async_copy(part_st.at[r], part_ref.at[l * 4 + g], out_sem.at[2 + r])
        copy.start()
        part_copies.append(copy)

    for copy in dg_copies:
        copy.wait_recv()
    bases = [role_expert_base(r) for r in range(N_DEV)]
    row_iota = lax.broadcasted_iota(jnp.int32, (LOC_E, N_TOK), 0)
    for j in range(TOP_K):
        want = ma[0, j:j + 1, :]
        acc = jnp.zeros((LOC_E, N_TOK), F32)
        for r in range(N_DEV):
            acc = jnp.where(want == (row_iota + bases[r]).astype(F32), dg_in[r] if r else dg_out[0], acc)
        dgate_ref[pl.ds(j, 1), :] = jnp.sum(acc, axis=0, keepdims=True)

    for e in (LOC_E - 2, LOC_E - 1):
        for copy in st_copies(e):
            copy.wait()
    for copy in [us_copy, xs_copy] + part_copies:
        copy.wait()
    for copy in sends + metas + dg_copies:
        copy.wait_send()


def front(x_rows, dy_rows, meta, w_gate, w_up, w_down):
    dma = pltpu.SemaphoreType.DMA
    return pl.pallas_call(
        front_kernel,
        out_shape=[jax.ShapeDtypeStruct((N_DEV, N_TOK, D), BF16), jax.ShapeDtypeStruct((TOP_K, N_TOK), F32),
                   jax.ShapeDtypeStruct((LOC_E, SLOTS, D), BF16), jax.ShapeDtypeStruct((LOC_E, SLOTS, D), BF16),
                   jax.ShapeDtypeStruct((LOC_E, SLOTS, F), BF16), jax.ShapeDtypeStruct((LOC_E, SLOTS, 2 * F), BF16)],
        in_specs=[ANY] * 6, out_specs=[ANY, VMEM] + [ANY] * 4,
        scratch_shapes=[
            pltpu.VMEM((N_DEV, N_TOK, D), BF16), pltpu.VMEM((N_DEV, N_TOK, D), BF16), pltpu.VMEM((N_DEV, 2 * TOP_K, N_TOK), F32),
            pltpu.VMEM((LOC_E, SLOTS, D), BF16), pltpu.VMEM((LOC_E, 2 * SLOTS, D), BF16), pltpu.VMEM((N_PAIR, PAIR_ROWS, D), BF16),
            pltpu.VMEM((N_DEV, LOC_E * CAP, N_TOK), BF16), pltpu.VMEM((N_DEV, LOC_E, CAP, 128), F32), pltpu.VMEM((N_DEV, LOC_E, N_TOK), F32),
            pltpu.VMEM((LOC_E, 2 * SLOTS, F), F32), pltpu.VMEM((LOC_E, SLOTS, 128), F32),
            pltpu.VMEM((RING, F, D), BF16), pltpu.VMEM((RING, D, 2 * F), BF16), pltpu.VMEM((2, SLOTS, F), BF16), pltpu.VMEM((2, SLOTS, 2 * F), BF16),
            pltpu.VMEM((N_DEV, LOC_E, N_TOK), F32), pltpu.VMEM((N_DEV, LOC_E, N_TOK), F32), pltpu.VMEM((N_DEV, N_TOK, D), BF16),
            dma((40,)), dma((2, N_DEV, 2)), dma((N_DEV,)), dma((N_DEV,)), dma((N_DEV,)), dma((N_DEV,)), dma((3,)),
            dma((RING,)), dma((RING, 2)), dma((2, 2)), dma((2 + N_DEV,))],
        compiler_params=pltpu.CompilerParams(collective_id=0, has_side_effects=True, vmem_limit_bytes=63 * 1024 * 1024),
        name='front',
    )(x_rows, dy_rows, meta, w_gate, w_up, w_down)


def wgrad_kernel(x_ref, u_ref, hid_ref, dab_ref, dwg_ref, dwu_ref, dwd_ref):
    dwd_ref[0] = dot(hid_ref[0], u_ref[0], 0, 0).astype(BF16)
    both = dot(x_ref[0], dab_ref[0], 0, 0).astype(BF16)
    dwg_ref[0] = both[:, :F]
    dwu_ref[0] = both[:, F:]


def wgrad(xs, us, hid, dab):
    each = lambda *shape: pl.BlockSpec((1,) + shape, lambda e: (e, 0, 0))
    return pl.pallas_call(
        wgrad_kernel,
        grid=(LOC_E,),
        out_shape=[jax.ShapeDtypeStruct((LOC_E, D, F), BF16), jax.ShapeDtypeStruct((LOC_E, D, F), BF16), jax.ShapeDtypeStruct((LOC_E, F, D), BF16)],
        in_specs=[each(SLOTS, D), each(SLOTS, D), each(SLOTS, F), each(SLOTS, 2 * F)],
        out_specs=[each(D, F), each(D, F), each(F, D)],
        compiler_params=pltpu.CompilerParams(vmem_limit_bytes=60 * 1024 * 1024, dimension_semantics=('arbitrary',)),
        cost_estimate=pl.CostEstimate(flops=2 * LOC_E * SLOTS * D * F * 3, bytes_accessed=57_000_000, transcendentals=0),
        name='wgrad',
    )(xs, us, hid, dab)


def final_kernel(parts_ref, dx_ref):
    @pl.loop(0, N_TOK // 16)
    def _(i):
        rows = pl.ds(pl.multiple_of(i * 16, 16), 16)
        total = jnp.zeros((16, D), F32)
        for g in range(4):
            total += (parts_ref[g, rows].astype(F32) + parts_ref[4 + g, rows].astype(F32)).astype(BF16).astype(F32)
        dx_ref[rows] = total.astype(BF16)


def final_sum(parts):
    return pl.pallas_call(
        final_kernel,
        out_shape=jax.ShapeDtypeStruct((N_TOK, D), BF16),
        in_specs=[VMEM],
        out_specs=VMEM,
        compiler_params=pltpu.CompilerParams(vmem_limit_bytes=16 * 1024 * 1024),
        name='final_sum',
    )(parts)


def solution(mesh):
    spec = P(('part', 'grp', 'loc'))

    def device_step(x_rows, dy_rows, expert_ids, gate_vals, w_gate, w_up, w_down):
        meta = jnp.concatenate([expert_ids.T.astype(F32), gate_vals.T], axis=0)
        part, dgate_t, xs, us, hid, dab = front(x_rows, dy_rows, meta, w_gate, w_up, w_down)
        parts = lax.all_to_all(part, ('loc', 'grp'), 0, 0)
        dwg, dwu, dwd = wgrad(xs, us, hid, dab)
        return final_sum(parts), dgate_t.T, dwg, dwu, dwd

    return jax.shard_map(device_step, mesh=mesh, in_specs=(spec,) * 7, out_specs=(spec,) * 5, check_vma=False)
```

time: 660 us -> 112 us (0.17); the launches traced: 652 us -> 111 us
  other arithmetic: 176 us -> 2.01 us
  local copies, waits for them, and re-layouts: 148 us -> 0.6 us
  matrix products: 108 us -> 0 us
  Pallas kernels: 0 us -> 93.5 us
  waiting for transfers between devices: 96.2 us -> 11.9 us
  blocking collectives: 79.9 us -> 0 us
  starting transfers between devices: 42.7 us -> 2.4 us
    scatter-add x6 -> x0, other arithmetic: 120 us -> none  [the longest x2 54.2 us: slot_table(): jax.ops.segment_sum(jnp.ones_like(bin_ids), bin_ids, num_segments=num_bin...]
    dot_general x9 -> x0, matrix products: 108 us -> none  [the longest x1 13.8 us: expert_backward(): jnp.einsum(tr_form, d_pre_gate, w_gate, preferred_element_type=jnp.float32)]
    gather x15 -> x0, local copies, waits for them, and re-layouts: 99.8 us -> none  [the longest x10 55 us: gather_rows(): return jnp.take(source, row_index, axis=0, mode='fill', fill_value=fill_val)]
    pallas_call x0 -> x3, Pallas kernels: none -> 93.5 us  [the longest x1 66.3 us: front(): pl.pallas_call(front_kernel, out_shape=[jax.ShapeDtypeStruct((N_DEV, N_TO...]
    all_to_all x10 -> x1, waiting for transfers between devices: 96.2 us -> 11.9 us  [device_step(): parts = lax.all_to_all(part, ('loc', 'grp'), 0, 0)]
    all_to_all x1 -> x0, blocking collectives: 79.9 us -> none  [device_step(): lax.all_to_all(gather_rows(x_recv, fan_rows, 0).reshape(own_shape + (d_mo...]
    all_to_all x10 -> x1, starting transfers between devices: 42.7 us -> 2.4 us  [device_step(): parts = lax.all_to_all(part, ('loc', 'grp'), 0, 0)]
    scatter x2 -> x0, local copies, waits for them, and re-layouts: 29.2 us -> none  [slot_table(): jnp.full((num_bins * capacity + 1,), n_items, jnp.int32).at[dest_slot]]
  transfers between devices with their start and end apart: 10 -> 1, of which waited for: 3 -> 1; matrix products, arithmetic and copies ran while one was open for 50% -> 0% of each run, Pallas kernels for 0% -> 23%
where the time goes in v2:
time: 112 us; the launch traced here: 111 us
  Pallas kernels  93.5 us (83%)
  waiting for transfers between devices  11.9 us (11%)
  starting transfers between devices  2.4 us (2%)
  other arithmetic  2.01 us (2%)
    pallas_call x1, Pallas kernels, front(): pl.pallas_call(front_kernel, out_shape=[jax.ShapeDtypeStruct((N_DEV, N_TO...  66.3 us
    pallas_call x1, Pallas kernels, wgrad(): pl.pallas_call(wgrad_kernel, grid=(LOC_E,), out_shape=[jax.ShapeDtypeStru...  25.8 us
    all_to_all x1, waiting for transfers between devices, device_step(): parts = lax.all_to_all(part, ('loc', 'grp'), 0, 0)  11.9 us
    all_to_all x1, starting transfers between devices, device_step(): parts = lax.all_to_all(part, ('loc', 'grp'), 0, 0)  2.4 us
  transfers between devices with their start and end apart: 1, of which 1 were waited for; matrix products, arithmetic and copies ran while one was open for 0% of the time, Pallas kernels for 23%

profile of v2, /device:TPU:0, one launch (start us, length us, event | category | flops | bytes accessed | tf_op | source)
XLA Modules:
  0.0 111.1 jit_solution(1708086259116999044)
XLA Ops:
  0.6 0.7 convert_bitcast_fusion
  1.3 1.3 %pad_maximum_fusion.meta_ref = f32[16,192]{1,0:T(8,128)} fusion(f32[8,192]{1,0:T(8,128)} %bitcast.5, f32[8,192]{1,0:T(8,128)S(1)} %convert_bitcast_fusion), kind=kLoop, calls=%fused_computation | loop fusion | flops 3072 | bytes 24576 | tf_op jit(solution)/shard_map/concatenate | solution.py:380
  2.6 66.3 %front.1 = (bf16[8,192,1024]{2,1,0:T(8,128)(2,1)}, f32[8,192]{1,0:T(8,128)}, bf16[16,192,1024]{2,1,0:T(8,128)(2,1)}, bf16[16,192,1024]{2,1,0:T(8,128)(2,1)}, bf1...) custom-call(bf16[192,1024]{1,0:T(8,128)(2,1)} %x_ref.1, bf16[192,1024]{1,0:T(8,128)(2,1)} %dy_ref.1, ...), custom_call_target="tpu_custom_call" | custom-call | tf_op jit(solution)/shard_map/front/pallas_call | solution.py:314
  68.9 2.4 %all-to-all-start = ((bf16[8,192,1024]{2,1,0:T(8,128)(2,1)}), bf16[8,192,1024]{2,1,0:T(8,128)(2,1)S(1)}, u32[]{:S(2)}, u32[]{:S(2)}) async-start(bf16[8,192,1024]{2,1,0:T(8,128)(2,1)} %get-tuple-element.14), calls=%async_computation | async-start | bytes 6291456 | tf_op jit(solution)/shard_map/all_to_all | solution.py:382
  71.3 0.0 copy-start
  71.3 25.8 %wgrad.1 = (bf16[16,1024,384]{2,1,0:T(8,128)(2,1)}, bf16[16,1024,384]{2,1,0:T(8,128)(2,1)}, bf16[16,384,1024]{2,1,0:T(8,128)(2,1)}) custom-call(bf16[16,192,1024]{2,1,0:T(8,128)(2,1)} %get-tuple-element.16.x_ref, bf16[16,192,1024]{2,1,0:T(8,128)(2,1)} %get-tuple-element.17.u_ref, bf16[16,192,384]{2,1,0:T(8,128)(2,1)} %get-tuple-element.18.hid_ref, ...), custom_call_target="tpu_custom_call" | custom-call | flops 7247757312 | bytes 57000000 | tf_op jit(solution)/shard_map/wgrad/pallas_call | solution.py:343
  97.2 11.9 %all-to-all-done.parts_ref = bf16[8,192,1024]{2,1,0:T(8,128)(2,1)S(1)} async-done(((bf16[8,192,1024]{2,1,0:T(8,128)(2,1)}), bf16[8,192,1024]{2,1,0:T(8,128)(2,1)S(1)}, u32[]{:S(2)}, u32[]{:S(2)}) %all-to-all-start) | async-done | bytes 3145760 | tf_op jit(solution)/shard_map/all_to_all | solution.py:382
  109.1 1.4 %final_sum.1 = bf16[192,1024]{1,0:T(8,128)(2,1)} custom-call(bf16[8,192,1024]{2,1,0:T(8,128)(2,1)S(1)} %all-to-all-done.parts_ref), custom_call_target="tpu_custom_call" | custom-call | tf_op jit(solution)/shard_map/final_sum/pallas_call | solution.py:366
  110.5 0.0 copy-done
  110.5 0.6 copy.13
Async XLA Ops:
  68.9 40.2 %all-to-all-start = ((bf16[8,192,1024]{2,1,0:T(8,128)(2,1)}), bf16[8,192,1024]{2,1,0:T(8,128)(2,1)S(1)}, u32[]{:S(2)}, u32[]{:S(2)}) async-start(bf16[8,192,1024]{2,1,0:T(8,128)(2,1)} %get-tuple-element.14), calls=%async_computation | async-start | bytes 6291456 | tf_op jit(solution)/shard_map/all_to_all | solution.py:382
  71.3 39.1 %copy-start = (f32[8,192]{1,0:T(8,128)S(1)}, f32[8,192]{1,0:T(8,128)}, u32[]{:S(2)}) copy-start(f32[8,192]{1,0:T(8,128)} %get-tuple-element.15) | copy-start | bytes 18436

commit v3 on v2

--- a/solution.py
+++ b/solution.py
@@ -18,6 +18,7 @@
 PAIR_ROWS = LOC_E * PAIR
 N_PAIR = N_DEV // 2
 RING = 4
+W_RING = 6
 MESH = pl.DeviceIdType.MESH
 F32 = jnp.float32
 BF16 = jnp.bfloat16
@@ -55,10 +56,10 @@
     return lax.broadcasted_iota(jnp.int32, (LOC_E, rows, N_TOK), 1).astype(F32)
 
 
-def front_kernel(x_ref, dy_ref, meta_ref, wg_ref, wu_ref, wd_ref,
+def front_kernel(x_ref, dy_ref, ids_ref, gates_ref, wg_ref, wu_ref, wd_ref,
                  part_ref, dgate_ref, xs_ref, us_ref, hid_ref, dab_ref,
-                 xa, dya, ma, xs, uds, cs, hots, gcols, ranks, back, dgs, wd_buf, w_buf, hid_st, dab_st, dg_out, dg_in, part_st,
-                 send_sem, recv_sem, meta_send, meta_recv, dg_send, dg_recv, own_sem, wd_sem, w_sem, st_sem, out_sem):
+                 xa, dya, ids_all, gates_all, xs, uds, cs, hots, gcols, ranks, back, dgs, wd_buf, w_buf, pre0, pre1, hid0, hid1, dab0, dab1, dg_out, dg_in,
+                 send_sem, recv_sem, ids_send, ids_recv, gates_send, gates_recv, dg_send, dg_recv, own_sem, wd_sem, w_sem, st_sem, out_sem):
     P_, X_, Y_ = 1, 2, 4
     data = (dya, xa)
     raw = (dy_ref, x_ref)
@@ -86,17 +87,17 @@
         return pltpu.make_async_copy(wd_ref.at[e], wd_buf.at[slot], wd_sem.at[slot])
 
     def w_copies(e):
-        slot = lax.rem(e, RING)
+        slot = lax.rem(e, W_RING)
         return (pltpu.make_async_copy(wg_ref.at[e], w_buf.at[slot, :, pl.ds(0, F)], w_sem.at[slot, 0]),
                 pltpu.make_async_copy(wu_ref.at[e], w_buf.at[slot, :, pl.ds(F, F)], w_sem.at[slot, 1]))
 
-    own = [pltpu.make_async_copy(meta_ref, ma.at[0], own_sem.at[0]), pltpu.make_async_copy(dy_ref, dya.at[0], own_sem.at[1]),
-           pltpu.make_async_copy(x_ref, xa.at[0], own_sem.at[2])]
+    own = [pltpu.make_async_copy(ids_ref, ids_all.at[0], own_sem.at[0]), pltpu.make_async_copy(dy_ref, dya.at[0], own_sem.at[1]),
+           pltpu.make_async_copy(x_ref, xa.at[0], own_sem.at[2]), pltpu.make_async_copy(gates_ref, gates_all.at[0], own_sem.at[3])]
     for copy in own:
         copy.start()
     for e in range(RING):
         wd_copy(e).start()
-    for e in range(RING):
+    for e in range(W_RING):
         for copy in w_copies(e):
             copy.start()
 
@@ -107,31 +108,34 @@
 
     metas = []
     for role in range(1, N_DEV):
-        copy = pltpu.make_async_remote_copy(
-            src_ref=meta_ref, dst_ref=ma.at[role], send_sem=meta_send.at[role], recv_sem=meta_recv.at[role],
-            device_id=role_id(role), device_id_type=MESH)
-        copy.start()
-        metas.append(copy)
+        for src, dst, send_s, recv_s in ((ids_ref, ids_all, ids_send, ids_recv), (gates_ref, gates_all, gates_send, gates_recv)):
+            copy = pltpu.make_async_remote_copy(
+                src_ref=src, dst_ref=dst.at[role], send_sem=send_s.at[role], recv_sem=recv_s.at[role],
+                device_id=role_id(role), device_id_type=MESH)
+            copy.start()
+            metas.append(copy)
     for k in range(2):
         send(0, k, 0, X_)
         send(0, 1 - k, 0, Y_)
         send(0, k, 0, P_)
     own[0].wait()
+    own[3].wait()
     for copy in metas:
         copy.wait_recv()
 
-    e_iota = (lax.broadcasted_iota(jnp.int32, (LOC_E, N_TOK), 0) + role_expert_base(0)).astype(F32)
+    e_iota = (lax.broadcasted_iota(jnp.int32, (LOC_E, N_TOK), 0) + role_expert_base(0))
     before = (lax.broadcasted_iota(jnp.int32, (N_TOK, N_TOK), 0) < lax.broadcasted_iota(jnp.int32, (N_TOK, N_TOK), 1)).astype(BF16)
 
     @pl.loop(0, N_DEV)
     def _(r):
         member = jnp.zeros((LOC_E, N_TOK), F32)
         gate = jnp.zeros((LOC_E, N_TOK), F32)
-        meta = ma[r]
+        ids = ids_all[r]
+        gates = gates_all[r]
         for j in range(TOP_K):
-            hit = meta[j:j + 1] == e_iota
+            hit = ids[j:j + 1] == e_iota
             member = jnp.where(hit, 1.0, member)
-            gate = jnp.where(hit, meta[TOP_K + j:TOP_K + j + 1], gate)
+            gate = jnp.where(hit, gates[j:j + 1], gate)
         rank = jnp.where(member > 0, dot(member.astype(BF16), before), -1000.0)
         ranks[r] = rank
         mask = rank[:, None, :] == slot_iota(CAP)
@@ -140,7 +144,7 @@
         hots[r] = jnp.where(mask, 1.0, 0.0).reshape(LOC_E * CAP, N_TOK).astype(BF16)
 
     def gather(a, q):
-        @pl.loop(0, 4)
+        @pl.loop(0, 4, unroll=4)
         def _(c):
             cols = pl.ds(pl.multiple_of(c * 256, 256), 256)
             rows = pl.ds(q * PAIR, PAIR)
@@ -222,46 +226,80 @@
     xs_copy = pltpu.make_async_copy(xs, xs_ref, out_sem.at[1])
     xs_copy.start()
 
-    def st_copies(e):
-        slot = lax.rem(e, 2)
-        return (pltpu.make_async_copy(hid_st.at[slot], hid_ref.at[e], st_sem.at[slot, 0]),
-                pltpu.make_async_copy(dab_st.at[slot], dab_ref.at[e], st_sem.at[slot, 1]))
-
-    @pl.loop(0, LOC_E)
-    def _(e):
-        slot = lax.rem(e, RING)
-        st = lax.rem(e, 2)
-        for copy in w_copies(e):
-            copy.wait()
-
-        @pl.when(e >= 2)
-        def _():
-            for copy in st_copies(e - 2):
-                copy.wait()
-
-        pre = dot(xs[e], w_buf[slot])
-        pre_gate = pre[:, :F]
-        pre_up = pre[:, F:]
+    pres, hids, dabs = (pre0, pre1), (hid0, hid1), (dab0, dab1)
+
+    def st_copies(e, b):
+        return (pltpu.make_async_copy(hids[b], hid_ref.at[e], st_sem.at[b, 0]),
+                pltpu.make_async_copy(dabs[b], dab_ref.at[e], st_sem.at[b, 1]))
+
+    def up_step(e, b):
+        pres[b][...] = dot(xs[e], w_buf[lax.rem(e, W_RING)])
+
+    def mid_step(e, b):
+        pre_gate = pres[b][:, :F]
+        pre_up = pres[b][:, F:]
         sig = jax.nn.sigmoid(pre_gate)
         silu = pre_gate * sig
         hidden = (silu * pre_up).astype(BF16)
         d_hidden = back[e, :SLOTS]
         dgs[e] = jnp.broadcast_to(jnp.sum(hidden.astype(F32) * back[e, SLOTS:], axis=1, keepdims=True), (SLOTS, 128))
-        d_up = (d_hidden * silu).astype(BF16)
-        d_gate = (d_hidden * pre_up * sig * (1.0 + pre_gate * (1.0 - sig))).astype(BF16)
-        hid_st[st] = hidden
-        dab = jnp.concatenate([d_gate, d_up], axis=1)
-        dab_st[st] = dab
-        for copy in st_copies(e):
-            copy.start()
-        c = dot(dab, w_buf[slot], 1, 1).astype(BF16)
+        hids[b][...] = hidden
+        dabs[b][:, :F] = (d_hidden * pre_up * sig * (1.0 + pre_gate * (1.0 - sig))).astype(BF16)
+        dabs[b][:, F:] = (d_hidden * silu).astype(BF16)
+
+    def c_step(e, b):
+        c = dot(dabs[b][...], w_buf[lax.rem(e, W_RING)], 1, 1).astype(BF16)
         for q in range(N_PAIR):
             cs[q, pl.ds(pl.multiple_of(e * PAIR, 16), PAIR), :] = c[q * PAIR:(q + 1) * PAIR]
 
-        @pl.when(e + RING < LOC_E)
+    def wait_all(copies):
+        for copy in copies:
+            copy.wait()
+
+    def start_all(copies):
+        for copy in copies:
+            copy.start()
+
+    wait_all(w_copies(0))
+    wait_all(w_copies(1))
+    up_step(0, 0)
+    up_step(1, 1)
+    mid_step(0, 0)
+    start_all(st_copies(0, 0))
+
+    @pl.loop(0, LOC_E // 2 - 1)
+    def _(i):
+        e = 2 * i + 1
+        wait_all(w_copies(e + 1))
+        wait_all(w_copies(e + 2))
+
+        @pl.when(i > 0)
         def _():
-            for copy in w_copies(e + RING):
-                copy.start()
+            wait_all(st_copies(e - 2, 1))
+
+        up_step(e + 1, 0)
+        mid_step(e, 1)
+        c_step(e - 1, 0)
+        start_all(st_copies(e, 1))
+        wait_all(st_copies(e - 1, 0))
+        up_step(e + 2, 1)
+        mid_step(e + 1, 0)
+        c_step(e, 1)
+        start_all(st_copies(e + 1, 0))
+
+        @pl.when(e + 5 < LOC_E)
+        def _():
+            start_all(w_copies(e + 5))
+
+        @pl.when(e + 6 < LOC_E)
+        def _():
+            start_all(w_copies(e + 6))
+
+    wait_all(st_copies(LOC_E - 3, 1))
+    mid_step(LOC_E - 1, 1)
+    c_step(LOC_E - 2, 0)
+    start_all(st_copies(LOC_E - 1, 1))
+    c_step(LOC_E - 1, 1)
 
     dg_copies = []
     for r in range(N_DEV):
@@ -275,6 +313,8 @@
             copy.start()
             dg_copies.append(copy)
 
+    for copy in sends:
+        copy.wait_send()
     part_copies = []
     for r in range(N_DEV):
         q, h = r // 2, r % 2
@@ -283,9 +323,9 @@
         hot = jnp.where(wide, 1.0, 0.0).reshape(PAIR_ROWS, N_TOK).astype(BF16)
         for c in range(4):
             cols = slice(c * 256, (c + 1) * 256)
-            part_st[r, :, cols] = dot(hot, cs[q, :, cols], 0, 0).astype(BF16)
+            xa[r, :, cols] = dot(hot, cs[q, :, cols], 0, 0).astype(BF16)
         g, l = role_coords(r)
-        copy = pltpu.make_async_copy(part_st.at[r], part_ref.at[l * 4 + g], out_sem.at[2 + r])
+        copy = pltpu.make_async_copy(xa.at[r], part_ref.at[l * 4 + g], out_sem.at[2 + r])
         copy.start()
         part_copies.append(copy)
 
@@ -294,41 +334,41 @@
     bases = [role_expert_base(r) for r in range(N_DEV)]
     row_iota = lax.broadcasted_iota(jnp.int32, (LOC_E, N_TOK), 0)
     for j in range(TOP_K):
-        want = ma[0, j:j + 1, :]
+        want = ids_all[0, j:j + 1, :]
         acc = jnp.zeros((LOC_E, N_TOK), F32)
         for r in range(N_DEV):
-            acc = jnp.where(want == (row_iota + bases[r]).astype(F32), dg_in[r] if r else dg_out[0], acc)
+            acc = jnp.where(want == row_iota + bases[r], dg_in[r] if r else dg_out[0], acc)
         dgate_ref[pl.ds(j, 1), :] = jnp.sum(acc, axis=0, keepdims=True)
 
-    for e in (LOC_E - 2, LOC_E - 1):
-        for copy in st_copies(e):
-            copy.wait()
+    wait_all(st_copies(LOC_E - 2, 0))
+    wait_all(st_copies(LOC_E - 1, 1))
     for copy in [us_copy, xs_copy] + part_copies:
         copy.wait()
-    for copy in sends + metas + dg_copies:
+    for copy in metas + dg_copies:
         copy.wait_send()
 
 
-def front(x_rows, dy_rows, meta, w_gate, w_up, w_down):
+def front(x_rows, dy_rows, ids_t, gates_t, w_gate, w_up, w_down):
     dma = pltpu.SemaphoreType.DMA
     return pl.pallas_call(
         front_kernel,
         out_shape=[jax.ShapeDtypeStruct((N_DEV, N_TOK, D), BF16), jax.ShapeDtypeStruct((TOP_K, N_TOK), F32),
                    jax.ShapeDtypeStruct((LOC_E, SLOTS, D), BF16), jax.ShapeDtypeStruct((LOC_E, SLOTS, D), BF16),
                    jax.ShapeDtypeStruct((LOC_E, SLOTS, F), BF16), jax.ShapeDtypeStruct((LOC_E, SLOTS, 2 * F), BF16)],
-        in_specs=[ANY] * 6, out_specs=[ANY, VMEM] + [ANY] * 4,
+        in_specs=[ANY] * 7, out_specs=[ANY, VMEM] + [ANY] * 4,
         scratch_shapes=[
-            pltpu.VMEM((N_DEV, N_TOK, D), BF16), pltpu.VMEM((N_DEV, N_TOK, D), BF16), pltpu.VMEM((N_DEV, 2 * TOP_K, N_TOK), F32),
+            pltpu.VMEM((N_DEV, N_TOK, D), BF16), pltpu.VMEM((N_DEV, N_TOK, D), BF16), pltpu.VMEM((N_DEV, TOP_K, N_TOK), jnp.int32), pltpu.VMEM((N_DEV, TOP_K, N_TOK), F32),
             pltpu.VMEM((LOC_E, SLOTS, D), BF16), pltpu.VMEM((LOC_E, 2 * SLOTS, D), BF16), pltpu.VMEM((N_PAIR, PAIR_ROWS, D), BF16),
             pltpu.VMEM((N_DEV, LOC_E * CAP, N_TOK), BF16), pltpu.VMEM((N_DEV, LOC_E, CAP, 128), F32), pltpu.VMEM((N_DEV, LOC_E, N_TOK), F32),
             pltpu.VMEM((LOC_E, 2 * SLOTS, F), F32), pltpu.VMEM((LOC_E, SLOTS, 128), F32),
-            pltpu.VMEM((RING, F, D), BF16), pltpu.VMEM((RING, D, 2 * F), BF16), pltpu.VMEM((2, SLOTS, F), BF16), pltpu.VMEM((2, SLOTS, 2 * F), BF16),
-            pltpu.VMEM((N_DEV, LOC_E, N_TOK), F32), pltpu.VMEM((N_DEV, LOC_E, N_TOK), F32), pltpu.VMEM((N_DEV, N_TOK, D), BF16),
-            dma((40,)), dma((2, N_DEV, 2)), dma((N_DEV,)), dma((N_DEV,)), dma((N_DEV,)), dma((N_DEV,)), dma((3,)),
-            dma((RING,)), dma((RING, 2)), dma((2, 2)), dma((2 + N_DEV,))],
+            pltpu.VMEM((RING, F, D), BF16), pltpu.VMEM((W_RING, D, 2 * F), BF16), pltpu.VMEM((SLOTS, 2 * F), F32), pltpu.VMEM((SLOTS, 2 * F), F32),
+            pltpu.VMEM((SLOTS, F), BF16), pltpu.VMEM((SLOTS, F), BF16), pltpu.VMEM((SLOTS, 2 * F), BF16), pltpu.VMEM((SLOTS, 2 * F), BF16),
+            pltpu.VMEM((N_DEV, LOC_E, N_TOK), F32), pltpu.VMEM((N_DEV, LOC_E, N_TOK), F32),
+            dma((40,)), dma((2, N_DEV, 2)), dma((N_DEV,)), dma((N_DEV,)), dma((N_DEV,)), dma((N_DEV,)), dma((N_DEV,)), dma((N_DEV,)), dma((4,)),
+            dma((RING,)), dma((W_RING, 2)), dma((2, 2)), dma((2 + N_DEV,))],
         compiler_params=pltpu.CompilerParams(collective_id=0, has_side_effects=True, vmem_limit_bytes=63 * 1024 * 1024),
         name='front',
-    )(x_rows, dy_rows, meta, w_gate, w_up, w_down)
+    )(x_rows, dy_rows, ids_t, gates_t, w_gate, w_up, w_down)
 
 
 def wgrad_kernel(x_ref, u_ref, hid_ref, dab_ref, dwg_ref, dwu_ref, dwd_ref):
@@ -377,8 +417,7 @@
     spec = P(('part', 'grp', 'loc'))
 
     def device_step(x_rows, dy_rows, expert_ids, gate_vals, w_gate, w_up, w_down):
-        meta = jnp.concatenate([expert_ids.T.astype(F32), gate_vals.T], axis=0)
-        part, dgate_t, xs, us, hid, dab = front(x_rows, dy_rows, meta, w_gate, w_up, w_down)
+        part, dgate_t, xs, us, hid, dab = front(x_rows, dy_rows, expert_ids.T, gate_vals.T, w_gate, w_up, w_down)
         parts = lax.all_to_all(part, ('loc', 'grp'), 0, 0)
         dwg, dwu, dwd = wgrad(xs, us, hid, dab)
         return final_sum(parts), dgate_t.T, dwg, dwu, dwd

time: 112 us -> 104 us (0.929)
  Pallas kernels: 93.5 us -> 88.1 us
  other arithmetic: 2.01 us -> 0 us
    pallas_call x1, Pallas kernels: 66.3 us -> 60.8 us  [front(): pl.pallas_call(front_kernel, out_shape=[jax.ShapeDtypeStruct((N_DEV, N_TO...]
    concatenate x1 -> x0, other arithmetic: 1.31 us -> none  [device_step(): meta = jnp.concatenate([expert_ids.T.astype(F32), gate_vals.T], axis=0)]
  transfers between devices with their start and end apart: 1 -> 1, of which waited for: 1 -> 1; matrix products, arithmetic and copies ran while one was open for 0% -> 0% of each run, Pallas kernels for 23% -> 25%
where the time goes in v3:
time: 104 us
  Pallas kernels  88.1 us (85%)
  waiting for transfers between devices  11.9 us (11%)
  starting transfers between devices  2.4 us (2%)
    pallas_call x1, Pallas kernels, front(): pl.pallas_call(front_kernel, out_shape=[jax.ShapeDtypeStruct((N_DEV, N_TO...  60.8 us
    pallas_call x1, Pallas kernels, wgrad(): pl.pallas_call(wgrad_kernel, grid=(LOC_E,), out_shape=[jax.ShapeDtypeStru...  25.8 us
    all_to_all x1, waiting for transfers between devices, device_step(): parts = lax.all_to_all(part, ('loc', 'grp'), 0, 0)  11.9 us
    all_to_all x1, starting transfers between devices, device_step(): parts = lax.all_to_all(part, ('loc', 'grp'), 0, 0)  2.4 us
  transfers between devices with their start and end apart: 1, of which 1 were waited for; matrix products, arithmetic and copies ran while one was open for 0% of the time, Pallas kernels for 25%

profile of v3, /device:TPU:0, one launch (start us, length us, event | category | flops | bytes accessed | tf_op | source)
XLA Modules:
  0.0 103.6 jit_solution(14638220879202140047)
XLA Ops:
  0.6 60.8 %front.1 = (bf16[8,192,1024]{2,1,0:T(8,128)(2,1)}, f32[8,192]{1,0:T(8,128)}, bf16[16,192,1024]{2,1,0:T(8,128)(2,1)}, bf16[16,192,1024]{2,1,0:T(8,128)(2,1)}, bf1...) custom-call(bf16[192,1024]{1,0:T(8,128)(2,1)} %x_ref.1, bf16[192,1024]{1,0:T(8,128)(2,1)} %dy_ref.1, ...), custom_call_target="tpu_custom_call" | custom-call | tf_op jit(solution)/shard_map/front/pallas_call | solution.py:353
  61.5 2.4 %all-to-all-start = ((bf16[8,192,1024]{2,1,0:T(8,128)(2,1)}), bf16[8,192,1024]{2,1,0:T(8,128)(2,1)S(1)}, u32[]{:S(2)}, u32[]{:S(2)}) async-start(bf16[8,192,1024]{2,1,0:T(8,128)(2,1)} %get-tuple-element.14), calls=%async_computation | async-start | bytes 6291456 | tf_op jit(solution)/shard_map/all_to_all | solution.py:421
  63.9 0.0 copy-start
  63.9 25.8 %wgrad.1 = (bf16[16,1024,384]{2,1,0:T(8,128)(2,1)}, bf16[16,1024,384]{2,1,0:T(8,128)(2,1)}, bf16[16,384,1024]{2,1,0:T(8,128)(2,1)}) custom-call(bf16[16,192,1024]{2,1,0:T(8,128)(2,1)} %get-tuple-element.16.x_ref, bf16[16,192,1024]{2,1,0:T(8,128)(2,1)} %get-tuple-element.17.u_ref, bf16[16,192,384]{2,1,0:T(8,128)(2,1)} %get-tuple-element.18.hid_ref, ...), custom_call_target="tpu_custom_call" | custom-call | flops 7247757312 | bytes 57000000 | tf_op jit(solution)/shard_map/wgrad/pallas_call | solution.py:383
  89.7 11.9 %all-to-all-done.parts_ref = bf16[8,192,1024]{2,1,0:T(8,128)(2,1)S(1)} async-done(((bf16[8,192,1024]{2,1,0:T(8,128)(2,1)}), bf16[8,192,1024]{2,1,0:T(8,128)(2,1)S(1)}, u32[]{:S(2)}, u32[]{:S(2)}) %all-to-all-start) | async-done | bytes 3145760 | tf_op jit(solution)/shard_map/all_to_all | solution.py:421
  101.7 1.4 %final_sum.1 = bf16[192,1024]{1,0:T(8,128)(2,1)} custom-call(bf16[8,192,1024]{2,1,0:T(8,128)(2,1)S(1)} %all-to-all-done.parts_ref), custom_call_target="tpu_custom_call" | custom-call | tf_op jit(solution)/shard_map/final_sum/pallas_call | solution.py:406
  103.0 0.0 copy-done
  103.0 0.6 copy.13
Async XLA Ops:
  61.5 40.2 %all-to-all-start = ((bf16[8,192,1024]{2,1,0:T(8,128)(2,1)}), bf16[8,192,1024]{2,1,0:T(8,128)(2,1)S(1)}, u32[]{:S(2)}, u32[]{:S(2)}) async-start(bf16[8,192,1024]{2,1,0:T(8,128)(2,1)} %get-tuple-element.14), calls=%async_computation | async-start | bytes 6291456 | tf_op jit(solution)/shard_map/all_to_all | solution.py:421
  63.9 39.1 %copy-start = (f32[8,192]{1,0:T(8,128)S(1)}, f32[8,192]{1,0:T(8,128)}, u32[]{:S(2)}) copy-start(f32[8,192]{1,0:T(8,128)} %get-tuple-element.15) | copy-start | bytes 18436
